TPU v7x, 16 devices: a whole 2x2x2 slice. The times are simulated.
16 devices in a mesh: dp: 2 (over z), ep: 8 (over y, x, core).
Axes of the slice: x: 2, y: 2, z: 2, core: 2. Of those that a mesh axis runs over, the one named last changes fastest.
Arguments:
- hidden: bfloat16 [1024, 2048], P(('dp', 'ep')), parts along dimension 0
- positions: int32 [1024], P(('dp', 'ep')), parts along dimension 0
- expert_ids: int32 [2, 1024, 8], P(None, ('dp', 'ep')), parts along dimension 1
- k_cache: bfloat16 [2, 1024, 16, 16, 128], P(None, ('dp', 'ep')), parts along dimension 1
- v_cache: bfloat16 [2, 1024, 16, 16, 128], P(None, ('dp', 'ep')), parts along dimension 1
- w_query: bfloat16 [2, 2048, 2048], replicated
- w_key: bfloat16 [2, 2048, 2048], replicated
- w_value: bfloat16 [2, 2048, 2048], replicated
- w_out: bfloat16 [2, 2048, 2048], replicated
- attn_gain: float32 [2, 2048], replicated
- q_gain: float32 [2, 2048], replicated
- k_gain: float32 [2, 2048], replicated
- mlp_gain: float32 [2, 2048], replicated
- w_router: bfloat16 [2048, 64], replicated
- w_gate: bfloat16 [64, 2048, 1024], P('ep')
- w_up: bfloat16 [64, 2048, 1024], P('ep')
- w_down: bfloat16 [64, 1024, 2048], P('ep')
Outputs:
- output 1: bfloat16 [1024, 2048], P(('dp', 'ep')), parts along dimension 0
- output 2: bfloat16 [2, 1024, 16, 16, 128], P(None, ('dp', 'ep')), parts along dimension 1
- output 3: bfloat16 [2, 1024, 16, 16, 128], P(None, ('dp', 'ep')), parts along dimension 1
There are 2 independent parts. A program takes and returns all parts, laid end to end along the dimension named above; an argument that names none is the same for every part.
All inputs are finite; a program needn't handle non-finite values.
Results may differ from a plain program's by a relative error of at most 0.02.
Values are sent between devices in bfloat16 or wider.
A program may use at most 1 GiB of HBM per device.

v0:
```python
import jax
import jax.numpy as jnp
from jax import lax
from jax.sharding import PartitionSpec as P

RMS_EPS = 1e-5
ROPE_BASE = 10000.0
CAP_FACTOR = 2


def rms_norm(values, gain_vec):
    values = values.astype(jnp.float32)
    inv_rms = lax.rsqrt(jnp.mean(values * values, axis=-1, keepdims=True) + RMS_EPS)
    return values * inv_rms * gain_vec.astype(jnp.float32)


def rope_rotate(values, positions):
    half_dim = values.shape[-1] // 2
    frequencies = ROPE_BASE ** (-jnp.arange(half_dim, dtype=jnp.float32) / half_dim)
    angles = positions.astype(jnp.float32)[:, None] * frequencies[None, :]
    angles = angles.reshape((angles.shape[0],) + (1,) * (values.ndim - 2) + (half_dim,))
    cosines = jnp.cos(angles)
    sines = jnp.sin(angles)
    first_half = values[..., :half_dim]
    second_half = values[..., half_dim:]
    return jnp.concatenate([first_half * cosines - second_half * sines, second_half * cosines + first_half * sines], axis=-1)


def attention_local(hidden, positions, k_layer, v_layer, w_query, w_key, w_value, w_out, attn_gain, q_gain, k_gain):
    seq_rows = hidden.shape[0]
    cache_len, kv_heads, head_dim = k_layer.shape[1:]
    head_group = w_query.shape[1] // head_dim // kv_heads
    normed = rms_norm(hidden, attn_gain).astype(jnp.bfloat16)
    q_heads = rms_norm(jnp.dot(normed, w_query, preferred_element_type=jnp.float32), q_gain)
    key_row = rms_norm(jnp.dot(normed, w_key, preferred_element_type=jnp.float32), k_gain)
    value_row = jnp.dot(normed, w_value, preferred_element_type=jnp.float32).astype(jnp.bfloat16)
    value_row = value_row.reshape(seq_rows, kv_heads, head_dim)
    q_heads = rope_rotate(q_heads.reshape(seq_rows, kv_heads, head_group, head_dim), positions).astype(jnp.bfloat16)
    key_row = rope_rotate(key_row.reshape(seq_rows, kv_heads, head_dim), positions).astype(jnp.bfloat16)
    score_scale = head_dim ** -0.5
    past_scores = jnp.einsum('bkgd,bskd->bkgs', q_heads, k_layer, preferred_element_type=jnp.float32) * score_scale
    before = (jnp.arange(cache_len)[None, :] < positions[:, None])[:, None, None, :]
    past_scores = jnp.where(before, past_scores, -1e30)
    new_score = jnp.einsum('clhe,cle->clh', q_heads, key_row, preferred_element_type=jnp.float32)[..., None] * score_scale
    peak_score = jnp.maximum(jnp.max(past_scores, axis=-1, keepdims=True), new_score)
    past_exp = jnp.exp(past_scores - peak_score)
    new_exp = jnp.exp(new_score - peak_score)
    prob_sum = jnp.sum(past_exp, axis=-1, keepdims=True) + new_exp
    past_prob = (past_exp / prob_sum).astype(jnp.bfloat16)
    new_prob = (new_exp / prob_sum).astype(jnp.bfloat16)
    mixed_out = jnp.einsum('bkgs,bskd->bkgd', past_prob, v_layer, preferred_element_type=jnp.float32)
    mixed_out = mixed_out + new_prob.astype(jnp.float32) * value_row.astype(jnp.float32)[:, :, None, :]
    mixed_out = mixed_out.astype(jnp.bfloat16).reshape(seq_rows, kv_heads * head_group * head_dim)
    hidden = (hidden.astype(jnp.float32) + jnp.dot(mixed_out, w_out, preferred_element_type=jnp.float32)).astype(jnp.bfloat16)
    return hidden, key_row, value_row


def dispatch_plan(routes, num_experts, capacity):
    seq_rows, top_k = routes.shape
    chosen = jnp.sum(routes[:, :, None] == jnp.arange(num_experts, dtype=jnp.int32)[None, None, :], axis=1, dtype=jnp.int32)
    ranks = jnp.cumsum(chosen, axis=0) - 1
    slot_ids = routes * capacity + jnp.take_along_axis(ranks, routes, axis=1)
    fillers = jnp.repeat(jnp.arange(seq_rows, dtype=jnp.int32), top_k)
    slot_owner = jnp.zeros((num_experts * capacity,), jnp.int32).at[slot_ids.reshape(-1)].set(fillers)
    return slot_ids, slot_owner


def moe_local(hidden, routes, mlp_gain, w_router, w_gate, w_up, w_down, groups):
    seq_rows, model_dim = hidden.shape
    num_experts = w_router.shape[1]
    local_experts = w_gate.shape[0]
    capacity = CAP_FACTOR * seq_rows * routes.shape[1] // num_experts
    normed = rms_norm(hidden, mlp_gain).astype(jnp.bfloat16)
    router_prob = jax.nn.softmax(jnp.dot(normed, w_router, preferred_element_type=jnp.float32), axis=-1)
    gate_vals = jnp.take_along_axis(router_prob, routes, axis=1)
    slot_ids, slot_owner = dispatch_plan(routes, num_experts, capacity)
    send_buf = jnp.take(normed, slot_owner, axis=0).reshape(groups, local_experts, capacity, model_dim)
    recv_buf = lax.all_to_all(send_buf, 'ep', 0, 0, tiled=True)
    gate_act = jnp.einsum('gecd,edf->egcf', recv_buf, w_gate, preferred_element_type=jnp.float32)
    up_act = jnp.einsum('gecd,edf->egcf', recv_buf, w_up, preferred_element_type=jnp.float32)
    act_vals = (jax.nn.silu(gate_act) * up_act).astype(jnp.bfloat16)
    expert_out = jnp.einsum('egcf,efd->gecd', act_vals, w_down, preferred_element_type=jnp.float32).astype(jnp.bfloat16)
    returned = lax.all_to_all(expert_out, 'ep', 0, 0, tiled=True).reshape(num_experts * capacity, model_dim)
    picked = jnp.take(returned, slot_ids, axis=0)
    moe_out = jnp.sum(gate_vals[:, :, None] * picked.astype(jnp.float32), axis=1)
    return (hidden.astype(jnp.float32) + moe_out).astype(jnp.bfloat16)


def solution(mesh):
    groups = mesh.shape['ep']
    batch_axes = ('dp', 'ep')

    def device_step(hidden, positions, expert_ids, k_cache, v_cache, w_query, w_key, w_value, w_out, attn_gain, q_gain, k_gain, mlp_gain, w_router, w_gate, w_up, w_down):
        key_rows = []
        value_rows = []
        for layer_idx in range(expert_ids.shape[0]):
            hidden, key_row, value_row = attention_local(hidden, positions, k_cache[layer_idx], v_cache[layer_idx], w_query[layer_idx], w_key[layer_idx], w_value[layer_idx], w_out[layer_idx], attn_gain[layer_idx], q_gain[layer_idx], k_gain[layer_idx])
            key_rows.append(key_row)
            value_rows.append(value_row)
            hidden = moe_local(hidden, expert_ids[layer_idx], mlp_gain[layer_idx], w_router, w_gate, w_up, w_down, groups)
        hit_mask = (jnp.arange(k_cache.shape[2])[None, :] == positions[:, None])[None, :, :, None, None]
        k_new = jnp.where(hit_mask, jnp.stack(key_rows)[:, :, None], k_cache)
        v_new = jnp.where(hit_mask, jnp.stack(value_rows)[:, :, None], v_cache)
        return hidden, k_new, v_new

    row_spec = P(batch_axes, None)
    cache_spec = P(None, batch_axes, None, None, None)
    full_spec = P()
    expert_spec = P('ep', None, None)
    in_specs = (row_spec, P(batch_axes), P(None, batch_axes, None), cache_spec, cache_spec, full_spec, full_spec, full_spec, full_spec, full_spec, full_spec, full_spec, full_spec, full_spec, expert_spec, expert_spec, expert_spec)
    return jax.shard_map(device_step, mesh=mesh, in_specs=in_specs, out_specs=(row_spec, cache_spec, cache_spec), check_vma=False)
```

profile of v0, /device:TPU:0, one launch (start us, length us, event | category | flops | bytes accessed | tf_op | source)
XLA Modules:
  0.0 453.6 jit_solution(15958183766124130910)
XLA Ops:
  16.8 5.0 %fusion.78 = bf16[64,2048]{1,0:T(8,128)(2,1)S(1)} fusion(bf16[2,2048,2048]{2,1,0:T(8,128)(2,1)} %param.32, bf16[64,2048]{1,0:T(8,128)(2,1)S(1)} %copy-done.10, f32[2048]{0:T(1024)S(1)} %bitcast.278, f32[64]{0:T(128)S(1)} %add_rsqrt_fusion.7), kind=kOutput, calls=%fused_computation.78 | convolution fusion | flops 537526272 | bytes 8921344 | tf_op jit(solution)/shard_map/dot_general | solution.py:36
  22.0 5.1 %multiply_reduce_fusion.6 = (f32[64]{0:T(128)S(1)}, f32[64,2048]{1,0:T(8,128)S(1)}) fusion(bf16[2,2048,2048]{2,1,0:T(8,128)(2,1)} %param.31, bf16[64,2048]{1,0:T(8,128)(2,1)S(1)} %copy-done.10, f32[2048]{0:T(1024)S(1)} %bitcast.279, f32[64]{0:T(128)S(1)} %add_rsqrt_fusion.7), kind=kOutput, calls=%fused_computation.125 | convolution fusion | flops 537657280 | bytes 9183744 | tf_op jit(solution)/shard_map/dot_general | solution.py:35
  27.3 5.1 %multiply_reduce_fusion.7 = (f32[64]{0:T(128)S(1)}, f32[64,2048]{1,0:T(8,128)S(1)}) fusion(bf16[2,2048,2048]{2,1,0:T(8,128)(2,1)} %param.30, bf16[64,2048]{1,0:T(8,128)(2,1)S(1)} %copy-done.10, f32[2048]{0:T(1024)S(1)} %bitcast.280, f32[64]{0:T(128)S(1)} %add_rsqrt_fusion.7), kind=kOutput, calls=%fused_computation.129 | convolution fusion | flops 537657280 | bytes 9183744 | tf_op jit(solution)/shard_map/dot_general | solution.py:34
  34.5 6.1 %slice_bitcast_fusion.1 = (bf16[64,16,16,128]{3,2,1,0:T(8,128)(2,1)}, bf16[64,16,16,128]{3,2,1,0:T(8,128)(2,1)S(1)}) fusion(bf16[2,64,16,16,128]{4,3,2,1,0:T(8,128)(2,1)} %param.28), kind=kLoop, calls=%fused_computation.60 | loop fusion | bytes 16777216 | tf_op jit(solution)/shard_map/squeeze | solution.py:97
  44.0 5.9 %slice_bitcast_fusion = (bf16[64,16,16,128]{3,2,1,0:T(8,128)(2,1)}, bf16[64,16,16,128]{3,2,1,0:T(8,128)(2,1)S(1)}) fusion(bf16[2,64,16,16,128]{4,3,2,1,0:T(8,128)(2,1)} %param.29), kind=kLoop, calls=%fused_computation.59 | loop fusion | bytes 16777216 | tf_op jit(solution)/shard_map/squeeze | solution.py:97
  51.4 5.1 %multiply_reduce_fusion.5 = (f32[64]{0:T(128)S(1)}, f32[64,2048]{1,0:T(8,128)S(1)}) fusion(bf16[2,2048,2048]{2,1,0:T(8,128)(2,1)} %param.33, bf16[8,8,16,128]{3,2,1,0:T(8,128)(2,1)S(1)} %bitcast.268, bf16[64,2048]{1,0:T(8,128)(2,1)S(1)} %copy-done.10), kind=kOutput, calls=%fused_computation.121 | convolution fusion | flops 537657280 | bytes 9437440 | tf_op jit(solution)/shard_map/dot_general | solution.py:54
  56.6 6.0 %gather_fusion.2 = bf16[1024,2048]{1,0:T(8,128)(2,1)} fusion(bf16[64,2048]{1,0:T(8,128)(2,1)S(1)} %multiply_convert_fusion.3, s32[1024]{0:T(1024)S(1)} %fusion.122), kind=kCustom, calls=%fused_computation.2.clone | custom fusion | bytes 8392704 | tf_op jit(solution)/shard_map/jit(_take)/gather | solution.py:77
  65.2 54.6 %all_to_all.20 = bf16[8,8,16,2048]{3,2,1,0:T(8,128)(2,1)} all-to-all(bf16[8,8,16,2048]{3,2,1,0:T(8,128)(2,1)S(1)} %bitcast.251), channel_id=1, replica_groups=mesh['dp'=2,'ep'=8] {'ep'}, dimensions={0} | all-to-all | bytes 8388608 | tf_op jit(solution)/shard_map/all_to_all | solution.py:78
  119.8 18.3 %fusion.6 = f32[8,8,16,1024]{3,2,1,0:T(8,128)} fusion(bf16[8,2048,1024]{2,1,0:T(8,128)(2,1)} %param.40, bf16[8,8,16,2048]{3,2,1,0:T(8,128)(2,1)} %all_to_all.20), kind=kOutput, calls=%fused_computation.16 | convolution fusion | flops 4294967296 | bytes 41943040 | tf_op jit(solution)/shard_map/gecd,edf->egcf/dot_general | solution.py:80
  138.1 16.1 %multiply_convert_fusion.1 = bf16[8,8,16,1024]{3,2,1,0:T(8,128)(2,1)S(1)} fusion(f32[8,8,16,1024]{3,2,1,0:T(8,128)} %fusion.6, bf16[8,2048,1024]{2,1,0:T(8,128)(2,1)} %param.39, bf16[8,8,16,2048]{3,2,1,0:T(8,128)(2,1)} %all_to_all.20), kind=kOutput, calls=%fused_computation.63 | convolution fusion | flops 4301258752 | bytes 44040192 | tf_op jit(solution)/shard_map/gecd,edf->egcf/dot_general | solution.py:79
  154.2 17.1 %convert_bitcast_fusion.1 = bf16[8,8,16,2048]{3,2,0,1:T(8,128)(2,1)} fusion(bf16[8,8,16,1024]{3,2,1,0:T(8,128)(2,1)S(1)} %multiply_convert_fusion.1, bf16[8,1024,2048]{2,1,0:T(8,128)(2,1)} %param.41), kind=kOutput, calls=%fused_computation.62 | convolution fusion | flops 4297064448 | bytes 39845888 | tf_op jit(solution)/shard_map/egcf,efd->gecd/dot_general | solution.py:82
  188.0 41.6 %all-to-all-done.1 = bf16[8,8,16,2048]{3,2,1,0:T(8,128)(2,1)} async-done(((bf16[8,8,16,2048]{3,2,1,0:T(8,128)(2,1)}), bf16[8,8,16,2048]{3,2,1,0:T(8,128)(2,1)}, u32[]{:S(2)}, u32[]{:S(2)}) %all-to-all-start.1) | async-done | bytes 4194336 | tf_op jit(solution)/shard_map/all_to_all | solution.py:83
  229.6 7.3 %gather_fusion.3 = bf16[512,2048]{1,0:T(8,128)(2,1)S(1)} fusion(bf16[1024,2048]{1,0:T(8,128)(2,1)} %bitcast.29, s32[1024]{0:T(1024)S(1)} %pad_clamp_fusion.1), kind=kCustom, calls=%fused_computation.3.clone | custom fusion | bytes 4196352 | tf_op jit(solution)/shard_map/jit(_take)/gather | solution.py:84
  244.6 5.1 %multiply_reduce_fusion.3 = (f32[64]{0:T(128)S(1)}, f32[64,2048]{1,0:T(8,128)S(1)}) fusion(bf16[2,2048,2048]{2,1,0:T(8,128)(2,1)} %param.31, bf16[64,2048]{1,0:T(8,128)(2,1)S(1)} %get-tuple-element.10, f32[2048]{0:T(1024)S(1)} %bitcast.276, f32[64]{0:T(128)S(1)} %add_rsqrt_fusion.3), kind=kOutput, calls=%fused_computation.114 | convolution fusion | flops 537657280 | bytes 9183744 | tf_op jit(solution)/shard_map/dot_general | solution.py:35
  249.8 5.1 %multiply_reduce_fusion.4 = (f32[64]{0:T(128)S(1)}, f32[64,2048]{1,0:T(8,128)S(1)}) fusion(bf16[2,2048,2048]{2,1,0:T(8,128)(2,1)} %param.30, bf16[64,2048]{1,0:T(8,128)(2,1)S(1)} %get-tuple-element.10, f32[2048]{0:T(1024)S(1)} %bitcast.277, f32[64]{0:T(128)S(1)} %add_rsqrt_fusion.3), kind=kOutput, calls=%fused_computation.118 | convolution fusion | flops 537657280 | bytes 9183744 | tf_op jit(solution)/shard_map/dot_general | solution.py:34
  265.0 5.1 %multiply_reduce_fusion.2 = (f32[64]{0:T(128)S(1)}, f32[64,2048]{1,0:T(8,128)S(1)}) fusion(bf16[2,2048,2048]{2,1,0:T(8,128)(2,1)} %param.33, bf16[8,8,16,128]{3,2,1,0:T(8,128)(2,1)S(1)} %bitcast.267, bf16[64,2048]{1,0:T(8,128)(2,1)S(1)} %get-tuple-element.10), kind=kOutput, calls=%fused_computation.110 | convolution fusion | flops 537657280 | bytes 9437440 | tf_op jit(solution)/shard_map/dot_general | solution.py:54
  270.2 6.0 %gather_fusion.6 = bf16[1024,2048]{1,0:T(8,128)(2,1)} fusion(bf16[64,2048]{1,0:T(8,128)(2,1)S(1)} %multiply_convert_fusion.2, s32[1024]{0:T(1024)S(1)} %fusion.123), kind=kCustom, calls=%fused_computation.6.clone | custom fusion | bytes 8392704 | tf_op jit(solution)/shard_map/jit(_take)/gather | solution.py:77
  278.8 52.2 %all_to_all.21 = bf16[8,8,16,2048]{3,2,1,0:T(8,128)(2,1)} all-to-all(bf16[8,8,16,2048]{3,2,1,0:T(8,128)(2,1)S(1)} %bitcast.252), channel_id=1, replica_groups=mesh['dp'=2,'ep'=8] {'ep'}, dimensions={0} | all-to-all | bytes 8388608 | tf_op jit(solution)/shard_map/all_to_all | solution.py:78
  331.0 18.4 %fusion.4 = f32[8,8,16,1024]{3,2,1,0:T(8,128)} fusion(bf16[8,2048,1024]{2,1,0:T(8,128)(2,1)} %param.40, bf16[8,8,16,2048]{3,2,1,0:T(8,128)(2,1)} %all_to_all.21), kind=kOutput, calls=%fused_computation.14 | convolution fusion | flops 4294967296 | bytes 41943040 | tf_op jit(solution)/shard_map/gecd,edf->egcf/dot_general | solution.py:80
  349.4 17.2 %multiply_convert_fusion = bf16[8,8,16,1024]{3,2,1,0:T(8,128)(2,1)} fusion(f32[8,8,16,1024]{3,2,1,0:T(8,128)} %fusion.4, bf16[8,2048,1024]{2,1,0:T(8,128)(2,1)} %param.39, bf16[8,8,16,2048]{3,2,1,0:T(8,128)(2,1)} %all_to_all.21), kind=kOutput, calls=%fused_computation.58 | convolution fusion | flops 4301258752 | bytes 44040192 | tf_op jit(solution)/shard_map/gecd,edf->egcf/dot_general | solution.py:79
  366.6 17.7 %convert_bitcast_fusion = bf16[8,8,16,2048]{3,2,0,1:T(8,128)(2,1)} fusion(bf16[8,8,16,1024]{3,2,1,0:T(8,128)(2,1)} %multiply_convert_fusion, bf16[8,1024,2048]{2,1,0:T(8,128)(2,1)} %param.41), kind=kOutput, calls=%fused_computation.57 | convolution fusion | flops 4297064448 | bytes 39845888 | tf_op jit(solution)/shard_map/egcf,efd->gecd/dot_general | solution.py:82
  399.0 11.7 %broadcast_select_fusion = (bf16[2,64,16,16,128]{4,3,2,1,0:T(8,128)(2,1)}, bf16[2,64,16,16,128]{4,3,2,1,0:T(8,128)(2,1)}) fusion(bf16[2,64,16,16,128]{4,3,2,1,0:T(8,128)(2,1)} %param.29, pred[64,16]{1,0:T(8,128)(4,1)S(1)} %copy-done.12, bf16[2,64,16,128]{3,2,1,0:T(8,128)(2,1)S(1)} %pad_maximum_fusion, bf16[2,64,16,16,128]{4,3,2,1,0:T(8,128)(2,1)} %param.28, ...), kind=kLoop, calls=%fused_computation.46 | loop fusion | flops 8388608 | bytes 34604032 | tf_op jit(solution)/shard_map/jit(_where)/select_n | solution.py:103
  410.7 32.1 %all-to-all-done.3 = bf16[8,8,16,2048]{3,2,1,0:T(8,128)(2,1)} async-done(((bf16[8,8,16,2048]{3,2,1,0:T(8,128)(2,1)}), bf16[8,8,16,2048]{3,2,1,0:T(8,128)(2,1)}, u32[]{:S(2)}, u32[]{:S(2)}) %all-to-all-start.3) | async-done | bytes 4194336 | tf_op jit(solution)/shard_map/all_to_all | solution.py:83
  442.7 7.1 %gather_fusion.7 = bf16[512,2048]{1,0:T(8,128)(2,1)S(1)} fusion(bf16[1024,2048]{1,0:T(8,128)(2,1)} %bitcast.57, s32[1024]{0:T(1024)S(1)} %pad_clamp_fusion), kind=kCustom, calls=%fused_computation.7.clone | custom fusion | bytes 4196352 | tf_op jit(solution)/shard_map/jit(_take)/gather | solution.py:84
  (175 shorter events, 80.7 us)
Async XLA Ops:
  0.6 182.9 %copy-start = (bf16[2048,64]{0,1:T(8,128)(2,1)S(1)}, bf16[2048,64]{0,1:T(8,128)(2,1)}, u32[]{:S(2)}) copy-start(bf16[2048,64]{0,1:T(8,128)(2,1)} %param.38) | copy-start | bytes 786436
  4.6 3.8 copy-start.1
  9.1 4.0 copy-start.11
  9.1 7.3 %copy-start.10 = (bf16[64,2048]{1,0:T(8,128)(2,1)S(1)}, bf16[64,2048]{1,0:T(8,128)(2,1)}, u32[]{:S(2)}) copy-start(bf16[64,2048]{1,0:T(8,128)(2,1)} %param.25) | copy-start | bytes 786436
  9.1 7.5 %copy-start.13 = (f32[2,2048]{1,0:T(2,128)S(1)}, f32[2,2048]{1,0:T(2,128)}, u32[]{:S(2)}) copy-start(f32[2,2048]{1,0:T(2,128)} %param.34) | copy-start | bytes 49156
  9.1 7.5 %copy-start.14 = (f32[2,2048]{1,0:T(2,128)S(1)}, f32[2,2048]{1,0:T(2,128)}, u32[]{:S(2)}) copy-start(f32[2,2048]{1,0:T(2,128)} %param.35) | copy-start | bytes 49156
  9.2 7.5 %copy-start.15 = (f32[2,2048]{1,0:T(2,128)S(1)}, f32[2,2048]{1,0:T(2,128)}, u32[]{:S(2)}) copy-start(f32[2,2048]{1,0:T(2,128)} %param.36) | copy-start | bytes 49156
  9.2 7.5 %copy-start.16 = (f32[2,2048]{1,0:T(2,128)S(1)}, f32[2,2048]{1,0:T(2,128)}, u32[]{:S(2)}) copy-start(f32[2,2048]{1,0:T(2,128)} %param.37) | copy-start | bytes 49156
  21.8 5.3 %copy-start.8 = (bf16[64,2048]{1,0:T(8,128)(2,1)}, bf16[64,2048]{1,0:T(8,128)(2,1)S(1)}, u32[]{:S(2)}) copy-start(bf16[64,2048]{1,0:T(8,128)(2,1)S(1)} %fusion.78) | copy-start | bytes 786436
  33.2 0.7 copy-start.4
  33.2 0.8 copy-start.6
  176.1 53.6 %all-to-all-start.1 = ((bf16[8,8,16,2048]{3,2,1,0:T(8,128)(2,1)}), bf16[8,8,16,2048]{3,2,1,0:T(8,128)(2,1)}, u32[]{:S(2)}, u32[]{:S(2)}) async-start(bf16[8,8,16,2048]{3,2,1,0:T(8,128)(2,1)} %copy.63), calls=%async_computation.1 | async-start | bytes 8388608 | tf_op jit(solution)/shard_map/all_to_all | solution.py:83
  255.0 2.2 copy-start.3
  389.1 4.7 %copy-start.17 = (pred[64,8]{0,1:T(8,128)(4,1)S(1)}, pred[64,8]{0,1:T(8,128)(4,1)}, u32[]{:S(2)}) copy-start(pred[64,8]{0,1:T(8,128)(4,1)} %get-tuple-element.6) | copy-start | bytes 1540
  389.1 5.0 %copy-start.9 = (bf16[64,2048]{1,0:T(8,128)(2,1)S(1)}, bf16[64,2048]{1,0:T(8,128)(2,1)}, u32[]{:S(2)}) copy-start(bf16[64,2048]{1,0:T(8,128)(2,1)} %copy-done.8) | copy-start | bytes 786436
  389.1 5.4 %copy-start.2 = (s32[512]{0:T(512)S(1)}, s32[512]{0:T(512)}, u32[]{:S(2)}) copy-start(s32[512]{0:T(512)} %copy-done.1) | copy-start | bytes 6148
  389.1 53.7 %all-to-all-start.3 = ((bf16[8,8,16,2048]{3,2,1,0:T(8,128)(2,1)}), bf16[8,8,16,2048]{3,2,1,0:T(8,128)(2,1)}, u32[]{:S(2)}, u32[]{:S(2)}) async-start(bf16[8,8,16,2048]{3,2,1,0:T(8,128)(2,1)} %copy.76), calls=%async_computation.3 | async-start | bytes 8388608 | tf_op jit(solution)/shard_map/all_to_all | solution.py:83
  394.5 4.2 copy-start.5
  394.5 4.2 copy-start.7
  394.5 4.5 %copy-start.12 = (pred[64,16]{1,0:T(8,128)(4,1)S(1)}, pred[64,16]{1,0:T(8,128)(4,1)}, u32[]{:S(2)}) copy-start(pred[64,16]{1,0:T(8,128)(4,1)} %get-tuple-element.47) | copy-start | bytes 3076
where the time goes:
time: 461 us; the launch traced here: 454 us
  matrix products  155 us (34%)
  blocking collectives  107 us (23%)
  local copies, waits for them, and re-layouts  75.5 us (16%)
  waiting for transfers between devices  73.6 us (16%)
  other arithmetic  31.3 us (7%)
  starting transfers between devices  9.22 us (2%)
    all_to_all x2, blocking collectives, moe_local(): recv_buf = lax.all_to_all(send_buf, 'ep', 0, 0, tiled=True)  107 us
    all_to_all x2, waiting for transfers between devices, moe_local(): lax.all_to_all(expert_out, 'ep', 0, 0, tiled=True)  73.6 us
    dot_general x2, matrix products, moe_local(): jnp.einsum('gecd,edf->egcf', recv_buf, w_up, preferred_element_type=jnp.f...  36.7 us
    dot_general x2, matrix products, moe_local(): jnp.einsum('egcf,efd->gecd', act_vals, w_down, preferred_element_type=jnp...  34.9 us
    dot_general x2, matrix products, moe_local(): jnp.einsum('gecd,edf->egcf', recv_buf, w_gate, preferred_element_type=jnp...  33.3 us
    gather x2, local copies, waits for them, and re-layouts, moe_local(): picked = jnp.take(returned, slot_ids, axis=0)  14.4 us
    gather x2, local copies, waits for them, and re-layouts, moe_local(): jnp.take(normed, slot_owner, axis=0)  12 us
    select_n x1, other arithmetic, device_step(): v_new = jnp.where(hit_mask, jnp.stack(value_rows)[:, :, None], v_cache)  11.7 us
  transfers between devices with their start and end apart: 2, of which 2 were waited for; matrix products, arithmetic and copies ran while one was open for 5% of the time, Pallas kernels for 0%

commit v1 on v0

v1 whole, which is shorter than its diff:
```python
import functools

import jax
import jax.numpy as jnp
from jax import lax
from jax.experimental import pallas as pl
from jax.experimental.pallas import tpu as pltpu
from jax.sharding import PartitionSpec as P

RMS_EPS = 1e-5
ROPE_BASE = 10000.0
CAP = 16
SLOTS = 5
F32 = jnp.float32
BF16 = jnp.bfloat16
ANY = pl.BlockSpec(memory_space=pl.ANY)
VMEM = pl.BlockSpec(memory_space=pltpu.VMEM)
SMEM = pl.BlockSpec(memory_space=pltpu.SMEM)
MESH = pl.DeviceIdType.MESH
NT = (((1,), (1,)), ((), ()))


def rms_rows(values, gain_row):
    inv_rms = lax.rsqrt(jnp.mean(values * values, axis=-1, keepdims=True) + RMS_EPS)
    return values * inv_rms * gain_row


def attn_kernel(layer, pos_ref, x_ref, cos_ref, sin_ref, attn_gain, q_gain, k_gain, mlp_gain, router_ref, member_ref,
                wq, wk, wv, wo, k_in, v_in, *rest):
    if layer > 0:
        rest = rest[2:]
    (x1_ref, h2_ref, gt_ref, k_out, v_out,
     wbuf, kbuf, vbuf, h_buf, lin, q2d, k2d, v2d, o2d, mixed, wsem, csem, osem) = rest
    rows, dim = x_ref.shape
    heads, hd = k_in.shape[3], k_in.shape[4]
    cache_len = k_in.shape[2]
    half = dim // 2

    def wcopy(i):
        src = (wq, wk, wv, wo)[i // 2]
        return pltpu.make_async_copy(src.at[layer, :, pl.ds((i % 2) * half, half)], wbuf.at[i], wsem.at[i])

    kcopy = pltpu.make_async_copy(k_in.at[layer], kbuf, csem.at[0])
    vcopy = pltpu.make_async_copy(v_in.at[layer], vbuf, csem.at[1])
    for i in range(4):
        wcopy(i).start()
    kcopy.start()
    for i in range(4, 6):
        wcopy(i).start()
    vcopy.start()
    for i in range(6, 8):
        wcopy(i).start()

    x = x_ref[...].astype(F32)
    h_buf[...] = rms_rows(x, attn_gain[layer:layer + 1, :]).astype(BF16)
    cos = cos_ref[...]
    sin = sin_ref[...]

    def project(which):
        for j in range(2):
            wcopy(2 * which + j).wait()
            lin[:, j * half:(j + 1) * half] = jnp.dot(h_buf[...], wbuf[2 * which + j], preferred_element_type=F32)

    def spread(gain_ref, dst):
        values = lin[...]
        inv_rms = lax.rsqrt(jnp.mean(values * values, axis=-1, keepdims=True) + RMS_EPS)
        for h in range(heads):
            cols = slice(h * hd, (h + 1) * hd)
            part = lin[:, cols] * inv_rms * gain_ref[layer:layer + 1, cols]
            part = part * cos + pltpu.roll(part, hd // 2, 1) * sin
            dst[pl.ds(h, rows, stride=heads), :] = part

    project(0)
    spread(q_gain, q2d)
    project(1)
    spread(k_gain, k2d)
    project(2)
    for h in range(heads):
        v2d[pl.ds(h, rows, stride=heads), :] = lin[:, h * hd:(h + 1) * hd]
    kcopy.wait()
    vcopy.wait()

    span = cache_len * heads
    col = lax.broadcasted_iota(jnp.int32, (heads, span), 1)
    row = lax.broadcasted_iota(jnp.int32, (heads, span), 0)
    same_head = (col % heads) == row
    cache_row = jnp.where(same_head, col // heads, cache_len)
    scale = hd ** -0.5
    group = 8

    def out_copies(g):
        at = pl.ds(pl.multiple_of(g * group, group), group)
        return (pltpu.make_async_copy(kbuf.at[at], k_out.at[layer, at], osem.at[0, g]),
                pltpu.make_async_copy(vbuf.at[at], v_out.at[layer, at], osem.at[1, g]))

    def attend(g, carry):
        outs = []
        for i in range(group):
            b = g * group + i
            p = pos_ref[b]
            at = pl.ds(pl.multiple_of(b * heads, heads), heads)
            kbuf[b, p] = k2d[at, :].astype(BF16)
            vbuf[b, p] = v2d[at, :].astype(BF16)
            kmat = kbuf[b].reshape(span, hd)
            scores = lax.dot_general(q2d[at, :].astype(BF16), kmat, NT, preferred_element_type=F32) * scale
            valid = cache_row <= p
            scores = jnp.where(valid, scores, -1e30)
            peak = jnp.max(scores, axis=-1, keepdims=True)
            weight = jnp.where(valid, jnp.exp(scores - peak), 0.0)
            outs.append((weight / jnp.sum(weight, axis=-1, keepdims=True)).astype(BF16))
        for i in range(group):
            b = g * group + i
            at = pl.ds(pl.multiple_of(b * heads, heads), heads)
            o2d[at, :] = jnp.dot(outs[i], vbuf[b].reshape(span, hd), preferred_element_type=F32)

        @pl.when(g > 0)
        def _():
            for copy in out_copies(g - 1):
                copy.start()
        return carry

    groups = rows // group
    lax.fori_loop(0, groups, attend, 0)
    for h in range(heads):
        mixed[:, h * hd:(h + 1) * hd] = o2d[pl.ds(h, rows, stride=heads), :].astype(BF16)
    for copy in out_copies(groups - 1):
        copy.start()
    for j in range(2):
        cols = slice(j * half, (j + 1) * half)
        wcopy(6 + j).wait()
        lin[:, cols] = x_ref[:, cols].astype(F32) + jnp.dot(mixed[...], wbuf[6 + j], preferred_element_type=F32)
    x1 = lin[...].astype(BF16)
    x1_ref[...] = x1
    h2 = rms_rows(x1.astype(F32), mlp_gain[layer:layer + 1, :]).astype(BF16)
    h2_ref[...] = h2
    logits = lax.dot_general(router_ref[...], jnp.concatenate([h2, h2], axis=0), NT, preferred_element_type=F32)
    logits = jnp.exp(logits - jnp.max(logits, axis=0, keepdims=True))
    probs = logits / jnp.sum(logits, axis=0, keepdims=True)
    gt_ref[...] = jnp.where(member_ref[layer] > 0.5, probs, -1.0)
    for g in range(groups):
        for copy in out_copies(g):
            copy.wait()


def attention(layer, pos, x, cos, sin, attn_gain, q_gain, k_gain, mlp_gain, router_t, member, wq, wk, wv, wo, k_in, v_in, prev):
    rows, dim = x.shape
    _, _, cache_len, heads, hd = k_in.shape
    aliases = {} if prev is None else {16: 3, 17: 4}
    prev = () if prev is None else prev
    groups = rows // 8
    return pl.pallas_call(
        functools.partial(attn_kernel, layer),
        name="attn",
        out_shape=(
            jax.ShapeDtypeStruct((rows, dim), BF16),
            jax.ShapeDtypeStruct((rows, dim), BF16),
            jax.ShapeDtypeStruct(member.shape[1:], F32),
            jax.ShapeDtypeStruct(k_in.shape, BF16),
            jax.ShapeDtypeStruct(v_in.shape, BF16),
        ),
        in_specs=[SMEM] + [VMEM] * 9 + [ANY] * (6 + len(prev)),
        out_specs=(VMEM, VMEM, VMEM, ANY, ANY),
        scratch_shapes=[
            pltpu.VMEM((8, dim, dim // 2), BF16),
            pltpu.VMEM(k_in.shape[1:], BF16),
            pltpu.VMEM(v_in.shape[1:], BF16),
            pltpu.VMEM((rows, dim), BF16),
            pltpu.VMEM((rows, dim), F32),
            pltpu.VMEM((rows * heads, hd), F32),
            pltpu.VMEM((rows * heads, hd), F32),
            pltpu.VMEM((rows * heads, hd), F32),
            pltpu.VMEM((rows * heads, hd), F32),
            pltpu.VMEM((rows, dim), BF16),
            pltpu.SemaphoreType.DMA((8,)),
            pltpu.SemaphoreType.DMA((2,)),
            pltpu.SemaphoreType.DMA((2, groups)),
        ],
        input_output_aliases=aliases,
        compiler_params=pltpu.CompilerParams(vmem_limit_bytes=60 * 2 ** 20),
    )(pos, x, cos, sin, attn_gain, q_gain, k_gain, mlp_gain, router_t, member, wq, wk, wv, wo, k_in, v_in, *prev)


def moe_kernel(h2_ref, gt_ref, x1_ref, wg, wu, wd, out_ref,
               ring, xall, xe, act, ybuf, pick, chi, cmid, clo, part, dr, sbuf, rr, gtall,
               wsem, a_send, a_recv, d_send, d_recv, g_send, g_recv, p_send, p_recv, r_send, r_recv):
    rows, dim = h2_ref.shape
    experts, _, ffn = wg.shape
    slots = pick.shape[0] // experts
    tokens = xall.shape[0]
    blocks = out_ref.shape[1] // ybuf.shape[1]
    bcols = ybuf.shape[1]
    pairs = experts + blocks
    half_rows = ring.shape[2] // 2

    def start_experts(i, slot):
        pltpu.make_async_copy(wg.at[i], ring.at[slot, 0], wsem.at[slot, 0]).start()
        pltpu.make_async_copy(wu.at[i], ring.at[slot, 1], wsem.at[slot, 1]).start()

    def start_down(c, slot):
        cols = pl.ds(pl.multiple_of(c * bcols, bcols), bcols)
        for e in range(experts):
            part_of, quarter = e // 4, e % 4
            pltpu.make_async_copy(
                wd.at[e, :, cols],
                ring.at[slot, part_of, pl.ds((quarter // 2) * half_rows, half_rows), pl.ds((quarter % 2) * bcols, bcols)],
                wsem.at[slot, part_of]).start()

    def wait_weights(slot, part_of):
        pltpu.make_async_copy(wg.at[0], ring.at[slot, part_of], wsem.at[slot, part_of]).wait()

    for i in range(SLOTS):
        start_experts(i, i)

    me = lax.axis_index("ep")
    core = lax.rem(me, 2)
    chip = lax.div(me, 2)
    at_x = lax.rem(chip, 2)
    at_y = lax.div(chip, 2)

    def chip_at(r):
        cx = 1 - at_x if r % 2 else at_x
        cy = 1 - at_y if r // 2 else at_y
        return 2 * cy + cx

    def device_at(q):
        return 2 * chip_at(q // 2) + (1 - core if q % 2 else core)

    barrier = pltpu.get_barrier_semaphore()
    for q in range(1, 8):
        pl.semaphore_signal(barrier, inc=1, device_id={"ep": device_at(q)}, device_id_type=MESH)
    pl.semaphore_wait(barrier, 7)

    def rows_of(dev):
        return pl.ds(pl.multiple_of(dev * rows, rows), rows)

    def experts_of(dev):
        return pl.ds(pl.multiple_of(dev * experts, experts), experts)

    def remote(src, dst, send, recv, dev):
        return pltpu.make_async_remote_copy(src_ref=src, dst_ref=dst, send_sem=send, recv_sem=recv,
                                            device_id={"ep": dev}, device_id_type=MESH)

    partner = device_at(1)
    gates = [remote(gt_ref.at[experts_of(device_at(q))], gtall.at[me], g_send.at[q], g_recv.at[q], device_at(q))
             for q in range(1, 8)]
    across = [remote(h2_ref, xall.at[rows_of(me)], a_send.at[r], a_recv.at[r], device_at(2 * r)) for r in range(1, 4)]
    own = remote(h2_ref, xall.at[rows_of(me)], d_send.at[0], d_recv.at[0], partner)
    for copy in gates:
        copy.start()
    for copy in across:
        copy.start()
    own.start()
    xall[rows_of(me), :] = h2_ref[...]
    gtall[me] = gt_ref[experts_of(me), :]
    for copy in gates:
        copy.wait_recv()

    lane = lax.broadcasted_iota(jnp.int32, (experts, 2 * rows), 1)
    gate_rows = jnp.concatenate(
        [jnp.where(lane < rows, gtall[2 * j], gtall[2 * j + 1]) for j in range(tokens // (2 * rows))], axis=1)
    chosen = gate_rows >= 0.0
    upper = (lax.broadcasted_iota(jnp.int32, (tokens, tokens), 0)
             <= lax.broadcasted_iota(jnp.int32, (tokens, tokens), 1))
    counted = jnp.dot(jnp.where(chosen, 1.0, 0.0).astype(BF16), jnp.where(upper, 1.0, 0.0).astype(BF16),
                      preferred_element_type=F32)
    ranks = jnp.where(chosen, counted - 1.0, -1.0)
    slot_of = lax.broadcasted_iota(jnp.int32, (slots, tokens), 0).astype(F32)
    for e in range(experts):
        pick[e * slots:(e + 1) * slots, :] = jnp.where(slot_of == ranks[e:e + 1, :], 1.0, 0.0).astype(BF16)
    stacked = jnp.concatenate([gate_rows, ranks, jnp.zeros((128 - 2 * experts, tokens), F32)], axis=0)
    columns = jnp.transpose(stacked)
    slot_at = lax.broadcasted_iota(jnp.int32, (tokens, slots), 1).astype(F32)
    for e in range(experts):
        gated = jnp.where(slot_at == columns[:, experts + e:experts + e + 1], columns[:, e:e + 1], 0.0)
        at = slice(e * slots, (e + 1) * slots)
        high = gated.astype(BF16)
        rest = gated - high.astype(F32)
        middle = rest.astype(BF16)
        chi[:, at] = high
        cmid[:, at] = middle
        clo[:, at] = (rest - middle.astype(F32)).astype(BF16)

    passed = []
    for r in range(1, 4):
        across[r - 1].wait_recv()
        block = xall.at[rows_of(device_at(2 * r))]
        copy = remote(block, block, d_send.at[r], d_recv.at[r], partner)
        copy.start()
        passed.append(copy)
    own.wait_recv()
    for copy in passed:
        copy.wait_recv()

    def expert_step(e, carry):
        slot = lax.rem(e, SLOTS)
        at = pl.ds(pl.multiple_of(e * slots, slots), slots)
        xe[...] = jnp.dot(pick[at, :], xall[...], preferred_element_type=F32).astype(BF16)
        wait_weights(slot, 0)
        gate_act = jnp.dot(xe[...], ring[slot, 0], preferred_element_type=F32)
        wait_weights(slot, 1)
        up_act = jnp.dot(xe[...], ring[slot, 1], preferred_element_type=F32)
        act[at, :] = (jax.nn.silu(gate_act) * up_act).astype(BF16)

        @pl.when(e + SLOTS < experts)
        def _():
            start_experts(e + SLOTS, slot)

        @pl.when(jnp.logical_and(e + SLOTS >= experts, e + SLOTS < pairs))
        def _():
            start_down(e + SLOTS - experts, slot)
        return carry

    lax.fori_loop(0, experts, expert_step, 0)

    def pair_copy(c):
        return remote(part.at[lax.rem(c, 2), :, 1 - core], dr.at[c], p_send.at[c], p_recv.at[c], partner)

    def chip_copy(c, r):
        return remote(sbuf.at[c, chip_at(r)], rr.at[c, r - 1], r_send.at[c, r - 1], r_recv.at[c, r - 1], device_at(2 * r))

    def relay(c):
        copy = pair_copy(c)
        copy.wait_send()
        copy.wait_recv()
        sbuf[c] = part[lax.rem(c, 2), :, core] + dr[c]
        for r in range(1, 4):
            chip_copy(c, r).start()

    def block_step(c, carry):
        slot = lax.rem(experts + c, SLOTS)
        for e in range(experts):
            part_of, quarter = e // 4, e % 4
            if quarter == 0:
                wait_weights(slot, part_of)
            down = ring[slot, part_of, (quarter // 2) * half_rows:(quarter // 2 + 1) * half_rows,
                        (quarter % 2) * bcols:(quarter % 2 + 1) * bcols]
            ybuf[e * slots:(e + 1) * slots, :] = jnp.dot(
                act[e * slots:(e + 1) * slots, :], down, preferred_element_type=F32).astype(BF16)

        @pl.when(c > 0)
        def _():
            relay(c - 1)

        def combine(m, inner):
            at = pl.ds(pl.multiple_of(m * 2 * rows, 2 * rows), 2 * rows)
            total = jnp.dot(chi[at, :], ybuf[...], preferred_element_type=F32)
            total += jnp.dot(cmid[at, :], ybuf[...], preferred_element_type=F32)
            total += jnp.dot(clo[at, :], ybuf[...], preferred_element_type=F32)
            part[lax.rem(c, 2), m] = total.reshape(2, rows, bcols)
            return inner

        lax.fori_loop(0, tokens // (2 * rows), combine, 0)
        pair_copy(c).start()
        return carry

    lax.fori_loop(0, blocks, block_step, 0)
    relay(blocks - 1)
    for c in range(blocks):
        for r in range(1, 4):
            chip_copy(c, r).wait_recv()
        cols = slice(c * bcols, (c + 1) * bcols)
        total = sbuf[c, chip] + rr[c, 0] + rr[c, 1] + rr[c, 2]
        out_ref[:, cols] = (x1_ref[:, cols].astype(F32) + total).astype(BF16)
    for copy in gates + across + [own] + passed:
        copy.wait_send()
    for c in range(blocks):
        for r in range(1, 4):
            chip_copy(c, r).wait_send()


def moe(h2, gt, x1, wg, wu, wd, groups):
    rows, dim = h2.shape
    experts, _, ffn = wg.shape
    tokens = rows * groups
    slots = CAP * groups
    blocks = 4
    bcols = dim // blocks
    chips = groups // 2
    dma = pltpu.SemaphoreType.DMA
    return pl.pallas_call(
        moe_kernel,
        name="moe",
        out_shape=jax.ShapeDtypeStruct((rows, dim), BF16),
        in_specs=[VMEM] * 3 + [ANY] * 3,
        out_specs=VMEM,
        scratch_shapes=[
            pltpu.VMEM((SLOTS, 2, dim, ffn), BF16),
            pltpu.VMEM((tokens, dim), BF16),
            pltpu.VMEM((slots, dim), BF16),
            pltpu.VMEM((experts * slots, ffn), BF16),
            pltpu.VMEM((experts * slots, bcols), BF16),
            pltpu.VMEM((experts * slots, tokens), BF16),
            pltpu.VMEM((tokens, experts * slots), BF16),
            pltpu.VMEM((tokens, experts * slots), BF16),
            pltpu.VMEM((tokens, experts * slots), BF16),
            pltpu.VMEM((2, chips, 2, rows, bcols), F32),
            pltpu.VMEM((blocks, chips, rows, bcols), F32),
            pltpu.VMEM((blocks, chips, rows, bcols), F32),
            pltpu.VMEM((blocks, chips - 1, rows, bcols), F32),
            pltpu.VMEM((groups, experts, 2 * rows), F32),
            dma((SLOTS, 2)),
            dma((4,)), dma((4,)), dma((4,)), dma((4,)), dma((8,)), dma((8,)),
            dma((blocks,)), dma((blocks,)), dma((blocks, chips - 1)), dma((blocks, chips - 1)),
        ],
        compiler_params=pltpu.CompilerParams(collective_id=0, has_side_effects=True, vmem_limit_bytes=62 * 2 ** 20),
    )(h2, gt, x1, wg, wu, wd)


def solution(mesh):
    groups = mesh.shape['ep']
    batch_axes = ('dp', 'ep')

    def device_step(hidden, positions, expert_ids, k_cache, v_cache, w_query, w_key, w_value, w_out, attn_gain, q_gain, k_gain, mlp_gain, w_router, w_gate, w_up, w_down):
        hd = k_cache.shape[-1]
        half_dim = hd // 2
        frequencies = ROPE_BASE ** (-jnp.arange(half_dim, dtype=F32) / half_dim)
        angles = positions.astype(F32)[:, None] * frequencies[None, :]
        cosines = jnp.cos(angles)
        sines = jnp.sin(angles)
        cos = jnp.concatenate([cosines, cosines], axis=-1)
        sin = jnp.concatenate([-sines, sines], axis=-1)
        num_experts = w_router.shape[1]
        hits = expert_ids[:, None, :, :] == jnp.arange(num_experts, dtype=jnp.int32)[None, :, None, None]
        member = jnp.any(hits, axis=-1).astype(F32)
        member = jnp.concatenate([member, member], axis=-1)
        router_t = w_router.T
        caches = None
        for layer in range(expert_ids.shape[0]):
            x1, h2, gt, k_new, v_new = attention(layer, positions, hidden, cos, sin, attn_gain, q_gain, k_gain, mlp_gain, router_t, member,
                                                 w_query, w_key, w_value, w_out, k_cache, v_cache, caches)
            caches = (k_new, v_new)
            hidden = moe(h2, gt, x1, w_gate, w_up, w_down, groups)
        return hidden, caches[0], caches[1]

    row_spec = P(batch_axes, None)
    cache_spec = P(None, batch_axes, None, None, None)
    full_spec = P()
    expert_spec = P('ep', None, None)
    in_specs = (row_spec, P(batch_axes), P(None, batch_axes, None), cache_spec, cache_spec, full_spec, full_spec, full_spec, full_spec, full_spec, full_spec, full_spec, full_spec, full_spec, expert_spec, expert_spec, expert_spec)
    return jax.shard_map(device_step, mesh=mesh, in_specs=in_specs, out_specs=(row_spec, cache_spec, cache_spec), check_vma=False)
```

time: 461 us -> 181 us (0.39); the launches traced: 454 us -> 180 us
  Pallas kernels: 0 us -> 175 us
  matrix products: 155 us -> 0 us
  blocking collectives: 107 us -> 0 us
  local copies, waits for them, and re-layouts: 75.5 us -> 1.67 us
  waiting for transfers between devices: 73.6 us -> 0 us
  other arithmetic: 31.3 us -> 3.17 us
  starting transfers between devices: 9.22 us -> 0 us
    pallas_call x0 -> x4, Pallas kernels: none -> 175 us  [the longest x2 133 us: moe(): pl.pallas_call(moe_kernel, name='moe', out_shape=jax.ShapeDtypeStruct((ro...]
    dot_general x20 -> x0, matrix products: 155 us -> none  [the longest x2 36.7 us: moe_local(): jnp.einsum('gecd,edf->egcf', recv_buf, w_up, preferred_element_type=jnp.f...]
    all_to_all x2 -> x0, blocking collectives: 107 us -> none  [moe_local(): recv_buf = lax.all_to_all(send_buf, 'ep', 0, 0, tiled=True)]
    all_to_all x2 -> x0, waiting for transfers between devices: 73.6 us -> none  [moe_local(): lax.all_to_all(expert_out, 'ep', 0, 0, tiled=True)]
    gather x20 -> x0, local copies, waits for them, and re-layouts: 42.7 us -> none  [the longest x2 14.4 us: moe_local(): picked = jnp.take(returned, slot_ids, axis=0)]
    select_n x8 -> x0, other arithmetic: 17 us -> none  [the longest x1 11.7 us: device_step(): v_new = jnp.where(hit_mask, jnp.stack(value_rows)[:, :, None], v_cache)]
    squeeze x5 -> x0, local copies, waits for them, and re-layouts: 12.9 us -> none  [the longest x1 6.1 us: device_step(): k_cache[layer_idx]]
    convert_element_type x6 -> x0, local copies, waits for them, and re-layouts: 10.8 us -> none  [the longest x2 9.44 us: moe_local(): jnp.einsum('egcf,efd->gecd', act_vals, w_down, preferred_element_type=jnp...]
  transfers between devices with their start and end apart: 2 -> 0, of which waited for: 2 -> 0; matrix products, arithmetic and copies ran while one was open for 5% -> 0% of each run, Pallas kernels for 0% -> 0%
where the time goes in v1:
time: 181 us; the launch traced here: 180 us
  Pallas kernels  175 us (97%)
  other arithmetic  3.17 us (2%)
    pallas_call x2, Pallas kernels, moe(): pl.pallas_call(moe_kernel, name='moe', out_shape=jax.ShapeDtypeStruct((ro...  133 us
    pallas_call x2, Pallas kernels, attention(): pl.pallas_call(functools.partial(attn_kernel, layer), name='attn', out_sh...  42.2 us

profile of v1, /device:TPU:0, one launch (start us, length us, event | category | flops | bytes accessed | tf_op | source)
XLA Modules:
  0.0 180.3 jit_solution(14986645753952801354)
XLA Ops:
  0.6 0.7 convert_element_type.4
  1.3 0.9 fusion
  2.2 0.7 add_convert_fusion.member_ref
  2.9 0.2 fusion.1
  3.1 0.7 pad_maximum_fusion
  3.8 21.0 %attn.2 = (bf16[64,2048]{1,0:T(8,128)(2,1)}, bf16[64,2048]{1,0:T(8,128)(2,1)}, f32[64,128]{1,0:T(8,128)}, bf16[2,64,16,16,128]{4,3,2,1,0:T(8,128)(2,1)}, bf16[2,64,16,16,128]{4,3,2,1,0:T(8,128)(2,1)}) custom-call(s32[64]{0:T(128)} %pos_ref.3, bf16[64,2048]{1,0:T(8,128)(2,1)} %x_ref.1, f32[64,128]{1,0:T(8,128)} %get-tuple-element.26.cos_ref, ...), custom_call_target="tpu_custom_call" | custom-call | tf_op jit(solution)/shard_map/attn/pallas_call | solution.py:151
  24.8 68.1 %moe.2.x_ref = bf16[64,2048]{1,0:T(8,128)(2,1)} custom-call(bf16[64,2048]{1,0:T(8,128)(2,1)} %get-tuple-element.13.h2_ref, f32[64,128]{1,0:T(8,128)} %get-tuple-element.14.gt_ref, bf16[64,2048]{1,0:T(8,128)(2,1)} %get-tuple-element.15.x1_ref, bf16[8,2048,1024]{2,1,0:T(8,128)(2,1)} %wg.3, bf16[8,2048,1024]{2,1,0:T(8,128)(2,1)} %wu.3, bf16[8,1024,2048]{2,1,0:T(8,128)(2,1)} %wd.3), custom_call_target="tpu_custom_call" | custom-call | tf_op jit(solution)/shard_map/moe/pallas_call | solution.py:380
  92.9 21.3 %attn.3 = (bf16[64,2048]{1,0:T(8,128)(2,1)}, bf16[64,2048]{1,0:T(8,128)(2,1)}, f32[64,128]{1,0:T(8,128)}, bf16[2,64,16,16,128]{4,3,2,1,0:T(8,128)(2,1)}, bf16[2,64,16,16,128]{4,3,2,1,0:T(8,128)(2,1)}) custom-call(s32[64]{0:T(128)} %pos_ref.3, bf16[64,2048]{1,0:T(8,128)(2,1)} %moe.2.x_ref, ...), custom_call_target="tpu_custom_call", output_to_operand_aliasing={{3}: (16, {}), {4}: (17, {})} | custom-call | tf_op jit(solution)/shard_map/attn/pallas_call | solution.py:151
  114.2 64.5 %moe.3 = bf16[64,2048]{1,0:T(8,128)(2,1)} custom-call(bf16[64,2048]{1,0:T(8,128)(2,1)} %get-tuple-element.18.h2_ref, f32[64,128]{1,0:T(8,128)} %get-tuple-element.19.gt_ref, bf16[64,2048]{1,0:T(8,128)(2,1)} %get-tuple-element.20.x1_ref, bf16[8,2048,1024]{2,1,0:T(8,128)(2,1)} %wg.3, bf16[8,2048,1024]{2,1,0:T(8,128)(2,1)} %wu.3, bf16[8,1024,2048]{2,1,0:T(8,128)(2,1)} %wd.3), custom_call_target="tpu_custom_call" | custom-call | tf_op jit(solution)/shard_map/moe/pallas_call | solution.py:380
  178.6 1.7 copy.26
  (1 shorter events, 0.0 us)

commit v2 on v1

v2 whole, which is shorter than its diff:
```python
import functools
import math

import jax
import jax.numpy as jnp
from jax import lax
from jax.experimental import pallas as pl
from jax.experimental.pallas import tpu as pltpu
from jax.sharding import PartitionSpec as P

RMS_EPS = 1e-5
ROPE_BASE = 10000.0
CAP = 16
SLOTS = 5
FCOLS = 512
F32 = jnp.float32
BF16 = jnp.bfloat16
ANY = pl.BlockSpec(memory_space=pl.ANY)
VMEM = pl.BlockSpec(memory_space=pltpu.VMEM)
SMEM = pl.BlockSpec(memory_space=pltpu.SMEM)
MESH = pl.DeviceIdType.MESH
NT = (((1,), (1,)), ((), ()))


def rms_rows(values, gain_row):
    inv_rms = lax.rsqrt(jnp.mean(values * values, axis=-1, keepdims=True) + RMS_EPS)
    return values * inv_rms * gain_row


def attn_kernel(layer, pos_ref, x_hbm, ids_hbm, attn_gain_hbm, q_gain_hbm, k_gain_hbm, mlp_gain_hbm, router_hbm,
                wq, wk, wv, wo, k_in, v_in, *rest):
    if layer > 0:
        rest = rest[2:]
    (x1_ref, h2_ref, gt_ref, k_out, v_out,
     x_ref, ids_ref, attn_gain, q_gain, k_gain, mlp_gain, router_ref, angle,
     wbuf, kbuf, vbuf, h_buf, lin, q2d, k2d, probs, mixed, ssem, wsem, csem, osem) = rest
    rows, dim = x_ref.shape
    heads, hd = k_in.shape[3], k_in.shape[4]
    cache_len = k_in.shape[2]
    half = dim // 2
    experts = router_ref.shape[0]

    def wcopy(i):
        src = (wq, wk, wv, wo)[i // 2]
        return pltpu.make_async_copy(src.at[layer, :, pl.ds((i % 2) * half, half)], wbuf.at[i], wsem.at[i])

    kcopy = pltpu.make_async_copy(k_in.at[layer], kbuf, csem.at[0])
    vcopy = pltpu.make_async_copy(v_in.at[layer], vbuf, csem.at[1])
    small = [pltpu.make_async_copy(src, dst, ssem.at[n]) for n, (src, dst) in enumerate((
        (x_hbm, x_ref), (attn_gain_hbm, attn_gain), (ids_hbm, ids_ref), (q_gain_hbm, q_gain), (k_gain_hbm, k_gain),
        (mlp_gain_hbm, mlp_gain), (router_hbm, router_ref)))]
    for copy in small:
        copy.start()
    for i in range(4):
        wcopy(i).start(priority=1)
    after = {0: [kcopy], 1: [wcopy(4)], 2: [wcopy(5)], 3: [vcopy], 4: [wcopy(6)], 5: [wcopy(7)]}
    for copy in small:
        copy.wait()
    x = x_ref[...].astype(F32)
    h_buf[...] = rms_rows(x, attn_gain[layer:layer + 1, :]).astype(BF16)
    lane = lax.broadcasted_iota(jnp.int32, (1, hd), 1)
    exponent = (lane % (hd // 2)).astype(F32) / (hd // 2)
    frequencies = jnp.exp(exponent * -math.log(ROPE_BASE))
    for b in range(rows):
        angle[b:b + 1, :] = frequencies * pos_ref[b].astype(F32)
    angles = angle[...]
    cos = jnp.cos(angles)
    sin = jnp.where(lane < hd // 2, -1.0, 1.0) * jnp.sin(angles)
    expert_row = lax.broadcasted_iota(jnp.int32, (experts, 128), 0)
    wide_ids = jnp.concatenate([ids_ref[layer]] * (128 // rows), axis=1)
    hits = expert_row == wide_ids[0:1, :]
    for j in range(1, wide_ids.shape[0]):
        hits = jnp.logical_or(hits, expert_row == wide_ids[j:j + 1, :])
    member = jnp.where(hits, 1.0, 0.0)

    def project(which):
        for j in range(2):
            wcopy(2 * which + j).wait()
            for copy in after.get(2 * which + j, ()):
                copy.start(priority=1)
            lin[:, j * half:(j + 1) * half] = jnp.dot(h_buf[...], wbuf[2 * which + j], preferred_element_type=F32)

    def spread(gain_ref, dst):
        values = lin[...]
        inv_rms = lax.rsqrt(jnp.mean(values * values, axis=-1, keepdims=True) + RMS_EPS)
        for h in range(heads):
            cols = slice(h * hd, (h + 1) * hd)
            part = lin[:, cols] * inv_rms * gain_ref[layer:layer + 1, cols]
            part = part * cos + pltpu.roll(part, hd // 2, 1) * sin
            dst[pl.ds(h, rows, stride=heads), :] = part

    project(0)
    spread(q_gain, q2d)
    project(1)
    spread(k_gain, k2d)
    kcopy.wait()

    span = cache_len * heads
    col = lax.broadcasted_iota(jnp.int32, (heads, span), 1)
    row = lax.broadcasted_iota(jnp.int32, (heads, span), 0)
    same_head = (col % heads) == row
    cache_row = jnp.where(same_head, col // heads, cache_len)
    scale = hd ** -0.5
    group = 8
    groups = rows // group

    def out_copy(which, g):
        at = pl.ds(pl.multiple_of(g * group, group), group)
        src, dst = ((kbuf, k_out), (vbuf, v_out))[which]
        return pltpu.make_async_copy(src.at[at], dst.at[layer, at], osem.at[which, g])

    def heads_of(b):
        return pl.ds(pl.multiple_of(b * heads, heads), heads)

    def score(g, carry):
        for i in range(group):
            b = g * group + i
            p = pos_ref[b]
            kbuf[b, p] = k2d[heads_of(b), :].astype(BF16)
            kmat = kbuf[b].reshape(span, hd)
            scores = lax.dot_general(q2d[heads_of(b), :].astype(BF16), kmat, NT, preferred_element_type=F32) * scale
            valid = cache_row <= p
            scores = jnp.where(valid, scores, -1e30)
            peak = jnp.max(scores, axis=-1, keepdims=True)
            weight = jnp.where(valid, jnp.exp(scores - peak), 0.0)
            probs[heads_of(b), :] = (weight / jnp.sum(weight, axis=-1, keepdims=True)).astype(BF16)

        @pl.when(g > 0)
        def _():
            out_copy(0, g - 1).start()
        return carry

    lax.fori_loop(0, groups, score, 0)
    project(2)
    out_copy(0, groups - 1).start()
    v2d = q2d
    o2d = k2d
    for h in range(heads):
        v2d[pl.ds(h, rows, stride=heads), :] = lin[:, h * hd:(h + 1) * hd]
    vcopy.wait()

    def mix(g, carry):
        for i in range(group):
            b = g * group + i
            vbuf[b, pos_ref[b]] = v2d[heads_of(b), :].astype(BF16)
            o2d[heads_of(b), :] = jnp.dot(probs[heads_of(b), :], vbuf[b].reshape(span, hd), preferred_element_type=F32)

        @pl.when(g > 0)
        def _():
            out_copy(1, g - 1).start()
        return carry

    lax.fori_loop(0, groups, mix, 0)
    for h in range(heads):
        mixed[:, h * hd:(h + 1) * hd] = o2d[pl.ds(h, rows, stride=heads), :].astype(BF16)
    out_copy(1, groups - 1).start()
    for j in range(2):
        cols = slice(j * half, (j + 1) * half)
        wcopy(6 + j).wait()
        lin[:, cols] = x_ref[:, cols].astype(F32) + jnp.dot(mixed[...], wbuf[6 + j], preferred_element_type=F32)
    x1 = lin[...].astype(BF16)
    x1_ref[...] = x1
    h2 = rms_rows(x1.astype(F32), mlp_gain[layer:layer + 1, :]).astype(BF16)
    h2_ref[...] = h2
    logits = lax.dot_general(router_ref[...], jnp.concatenate([h2] * (128 // rows), axis=0), NT, preferred_element_type=F32)
    logits = jnp.exp(logits - jnp.max(logits, axis=0, keepdims=True))
    router_probs = logits / jnp.sum(logits, axis=0, keepdims=True)
    gt_ref[...] = jnp.where(member > 0.5, router_probs, -1.0)
    for g in range(groups):
        for which in range(2):
            out_copy(which, g).wait()


def attention(layer, pos, x, ids, attn_gain, q_gain, k_gain, mlp_gain, router_t, wq, wk, wv, wo, k_in, v_in, prev):
    rows, dim = x.shape
    _, _, cache_len, heads, hd = k_in.shape
    aliases = {} if prev is None else {14: 3, 15: 4}
    prev = () if prev is None else prev
    groups = rows // 8
    return pl.pallas_call(
        functools.partial(attn_kernel, layer),
        name="attn",
        out_shape=(
            jax.ShapeDtypeStruct((rows, dim), BF16),
            jax.ShapeDtypeStruct((rows, dim), BF16),
            jax.ShapeDtypeStruct((router_t.shape[0], 128), F32),
            jax.ShapeDtypeStruct(k_in.shape, BF16),
            jax.ShapeDtypeStruct(v_in.shape, BF16),
        ),
        in_specs=[SMEM] + [ANY] * (13 + len(prev)),
        out_specs=(VMEM, VMEM, VMEM, ANY, ANY),
        scratch_shapes=[
            *[pltpu.VMEM(a.shape, a.dtype) for a in (x, ids, attn_gain, q_gain, k_gain, mlp_gain, router_t)],
            pltpu.VMEM((rows, hd), F32),
            pltpu.VMEM((8, dim, dim // 2), BF16),
            pltpu.VMEM(k_in.shape[1:], BF16),
            pltpu.VMEM(v_in.shape[1:], BF16),
            pltpu.VMEM((rows, dim), BF16),
            pltpu.VMEM((rows, dim), F32),
            pltpu.VMEM((rows * heads, hd), F32),
            pltpu.VMEM((rows * heads, hd), F32),
            pltpu.VMEM((rows * heads, cache_len * heads), BF16),
            pltpu.VMEM((rows, dim), BF16),
            pltpu.SemaphoreType.DMA((7,)),
            pltpu.SemaphoreType.DMA((8,)),
            pltpu.SemaphoreType.DMA((2,)),
            pltpu.SemaphoreType.DMA((2, groups)),
        ],
        input_output_aliases=aliases,
        compiler_params=pltpu.CompilerParams(vmem_limit_bytes=60 * 2 ** 20),
    )(pos, x, ids, attn_gain, q_gain, k_gain, mlp_gain, router_t, wq, wk, wv, wo, k_in, v_in, *prev)


def moe_kernel(h2_hbm, gt_hbm, x1_hbm, wg, wu, wd, out_ref,
               h2_ref, gt_ref, x1_ref, ring, xall, xs, act, ybuf, pick, spread, terms, part, dr, sbuf, step1, step2, gtall,
               ssem, wsem, a_send, a_recv, f_send, f_recv, d_send, d_recv, g_send, g_recv, p_send, p_recv, u_send, u_recv, w_send, w_recv):
    rows, dim = h2_ref.shape
    experts, _, ffn = wg.shape
    groups = xs.shape[1] // CAP
    chips = groups // 2
    bcols = ybuf.shape[2]
    blocks = dim // bcols
    sub = bcols // 2
    pairs = experts + blocks
    half_rows = ring.shape[2] // 2
    hrows = rows // 2

    def start_experts(i, slot):
        pltpu.make_async_copy(wg.at[i], ring.at[slot, 0], wsem.at[slot, 0]).start(priority=1)
        pltpu.make_async_copy(wu.at[i], ring.at[slot, 1], wsem.at[slot, 1]).start(priority=1)

    def start_down(c, slot):
        cols = pl.ds(pl.multiple_of(c * bcols, bcols), bcols)
        for e in range(experts):
            part_of, quarter = e // 4, e % 4
            pltpu.make_async_copy(
                wd.at[e, :, cols],
                ring.at[slot, part_of, pl.ds((quarter // 2) * half_rows, half_rows), pl.ds((quarter % 2) * bcols, bcols)],
                wsem.at[slot, part_of]).start(priority=1)

    def wait_weights(slot, part_of):
        pltpu.make_async_copy(wg.at[0], ring.at[slot, part_of], wsem.at[slot, part_of]).wait()

    small = [pltpu.make_async_copy(src, dst, ssem.at[n]) for n, (src, dst) in enumerate((
        (h2_hbm, h2_ref), (gt_hbm, gt_ref), (x1_hbm, x1_ref)))]
    for copy in small:
        copy.start()
    for i in range(SLOTS):
        start_experts(i, i)

    me = lax.axis_index("ep")
    core = lax.rem(me, 2)
    chip = lax.div(me, 2)
    at_x = lax.rem(chip, 2)
    at_y = lax.div(chip, 2)

    def chip_at(r):
        cx = 1 - at_x if r % 2 else at_x
        cy = 1 - at_y if r // 2 else at_y
        return 2 * cy + cx

    def device_at(q):
        return 2 * chip_at(q // 2) + (1 - core if q % 2 else core)

    barrier = pltpu.get_barrier_semaphore()
    for q in range(1, 8):
        pl.semaphore_signal(barrier, inc=1, device_id={"ep": device_at(q)}, device_id_type=MESH)
    for copy in small:
        copy.wait()
    pl.semaphore_wait(barrier, 7)

    def rows_of(dev):
        return pl.ds(pl.multiple_of(dev * rows, rows), rows)

    def half_of(dev, k):
        return pl.ds(pl.multiple_of(dev * rows + k * hrows, hrows), hrows)

    def experts_of(dev):
        return pl.ds(pl.multiple_of(dev * experts, experts), experts)

    def remote(src, dst, send, recv, dev):
        return pltpu.make_async_remote_copy(src_ref=src, dst_ref=dst, send_sem=send, recv_sem=recv,
                                            device_id={"ep": dev}, device_id_type=MESH)

    partner = device_at(1)
    gates = [remote(gt_ref.at[experts_of(device_at(q))], gtall.at[me], g_send.at[q], g_recv.at[q], device_at(q))
             for q in range(1, 8)]

    def across(r, k):
        return remote(h2_ref.at[pl.ds(k * hrows, hrows)], xall.at[half_of(me, k)], a_send.at[r - 1, k], a_recv.at[r - 1, k],
                      device_at(2 * r))

    own = remote(h2_ref, xall.at[rows_of(me)], d_send.at[0, 0], d_recv.at[0, 0], partner)
    for copy in gates:
        copy.start()
    for r, k in ((1, 0), (2, 1), (1, 1), (2, 0)):
        across(r, k).start()
    own.start()
    xall[rows_of(me), :] = h2_ref[...]
    gtall[me] = gt_ref[experts_of(me), :]
    for copy in gates:
        copy.wait_recv()

    lane = lax.broadcasted_iota(jnp.int32, (experts, 2 * rows), 1)
    gate_rows = jnp.concatenate([jnp.where(lane < rows, gtall[2 * j], gtall[2 * j + 1]) for j in range(chips)], axis=0)
    chosen = gate_rows >= 0.0
    first = lax.broadcasted_iota(jnp.int32, (2 * rows, 2 * rows), 0)
    second = lax.broadcasted_iota(jnp.int32, (2 * rows, 2 * rows), 1)
    upper = jnp.logical_and(first <= second, first // rows == second // rows)
    counted = jnp.dot(jnp.where(chosen, 1.0, 0.0).astype(BF16), jnp.where(upper, 1.0, 0.0).astype(BF16),
                      preferred_element_type=F32)
    ranks = jnp.where(chosen, counted - 1.0, -1.0)
    slot_of = lax.broadcasted_iota(jnp.int32, (CAP, 2 * rows), 0).astype(F32)
    left = lax.broadcasted_iota(jnp.int32, (CAP, 2 * rows), 1) < rows
    width = experts * CAP
    for j in range(chips):
        for e in range(experts):
            line = slice(j * experts + e, j * experts + e + 1)
            hit = slot_of == ranks[line, :]
            at = slice(e * CAP, (e + 1) * CAP)
            pick[j, at, :] = jnp.where(jnp.logical_and(hit, left), 1.0, 0.0).astype(BF16)
            pick[j, width + e * CAP:width + (e + 1) * CAP, :] = jnp.where(
                jnp.logical_and(hit, jnp.logical_not(left)), 1.0, 0.0).astype(BF16)
            spread[j, at, :] = jnp.where(hit, gate_rows[line, :], 0.0)
    for j in range(chips):
        gated = jnp.transpose(spread[j])
        high = gated.astype(BF16)
        rest = gated - high.astype(F32)
        middle = rest.astype(BF16)
        low = (rest - middle.astype(F32)).astype(BF16)
        for k in range(2):
            for n, term in enumerate((high, middle, low)):
                terms[2 * j + k, n * rows:(n + 1) * rows, :] = term[k * rows:(k + 1) * rows, :]

    passed = [own]

    def hand_over(r, k):
        block = xall.at[half_of(device_at(2 * r), k)]
        copy = remote(block, block, d_send.at[r, k], d_recv.at[r, k], partner)
        copy.start()
        passed.append(copy)

    def forward(r, k):
        block = xall.at[half_of(device_at(2 * r), k)]
        return remote(block, block, f_send.at[k], f_recv.at[k], device_at(2 * (3 - r)))

    across(1, 0).wait_recv()
    ahead = [forward(1, 0)]
    ahead[0].start()
    hand_over(1, 0)
    across(2, 1).wait_recv()
    ahead.append(forward(2, 1))
    ahead[1].start()
    hand_over(2, 1)

    def take_rows(r):
        j = chip_at(r)
        chosen_rows = jnp.dot(pick[j], xall[pl.ds(pl.multiple_of(j * 2 * rows, 2 * rows), 2 * rows), :],
                              preferred_element_type=F32).astype(BF16)
        for k in range(2):
            for e in range(experts):
                xs[e, pl.ds(pl.multiple_of((2 * j + k) * CAP, CAP), CAP), :] = chosen_rows[k * width + e * CAP:k * width + (e + 1) * CAP, :]

    own.wait_recv()
    take_rows(0)
    across(1, 1).wait_recv()
    hand_over(1, 1)
    across(2, 0).wait_recv()
    hand_over(2, 0)
    passed[1].wait_recv()
    passed[3].wait_recv()
    take_rows(1)
    passed[2].wait_recv()
    passed[4].wait_recv()
    take_rows(2)
    for k in range(2):
        ahead[k].wait_recv()
        hand_over(3, k)
    passed[5].wait_recv()
    passed[6].wait_recv()
    take_rows(3)

    def expert_step(e, carry):
        slot = lax.rem(e, SLOTS)
        at = pl.ds(pl.multiple_of(e * groups * CAP, groups * CAP), groups * CAP)
        wait_weights(slot, 0)
        wait_weights(slot, 1)
        for n in range(ffn // FCOLS):
            cols = slice(n * FCOLS, (n + 1) * FCOLS)
            gate_act = jnp.dot(xs[e], ring[slot, 0, :, cols], preferred_element_type=F32)
            up_act = jnp.dot(xs[e], ring[slot, 1, :, cols], preferred_element_type=F32)
            act[at, cols] = (jax.nn.silu(gate_act) * up_act).astype(BF16)

        @pl.when(e + SLOTS < experts)
        def _():
            start_experts(e + SLOTS, slot)

        @pl.when(jnp.logical_and(e + SLOTS >= experts, e + SLOTS < pairs))
        def _():
            start_down(e + SLOTS - experts, slot)
        return carry

    lax.fori_loop(0, experts, expert_step, 0)

    def pair_copy(c):
        return remote(part.at[lax.rem(c, 2), :, 1 - core], dr.at[c], p_send.at[c], p_recv.at[c], partner)

    def first_copy(c, s, k):
        to = 1 + s
        return remote(sbuf.at[c, s, chip_at((to, 3)[k])], step1.at[c, s, k], u_send.at[c, s, k], u_recv.at[c, s, k],
                      device_at(2 * to))

    def second_copy(c, s):
        to = 2 - s
        return remote(sbuf.at[c, s, chip_at(to)], step2.at[c, s], w_send.at[c, s], w_recv.at[c, s], device_at(2 * to))

    def relay_pair(c):
        copy = pair_copy(c)
        copy.wait_send()
        copy.wait_recv()
        both = part[lax.rem(c, 2), :, core] + dr[c]
        for s in range(2):
            sbuf[c, s] = both[:, :, s * sub:(s + 1) * sub]
        for k in (1, 0):
            for s in range(2):
                first_copy(c, s, k).start()

    def relay_first(c):
        for s in range(2):
            first_copy(c, s, 1).wait_recv()
            to = chip_at(2 - s)
            sbuf[c, s, to] = sbuf[c, s, to] + step1[c, s, 1]
            second_copy(c, s).start()

    def finish(c):
        for s in range(2):
            first_copy(c, s, 0).wait_recv()
            second_copy(c, s).wait_recv()
            cols = pl.ds(pl.multiple_of(c * bcols + s * sub, sub), sub)
            total = sbuf[c, s, chip] + step1[c, s, 0] + step2[c, s]
            out_ref[:, cols] = (x1_ref[:, cols].astype(F32) + total).astype(BF16)

    def block_step(c, carry):
        slot = lax.rem(experts + c, SLOTS)

        @pl.when(c < blocks)
        def _():
            for e in range(experts):
                part_of, quarter = e // 4, e % 4
                if quarter == 0:
                    wait_weights(slot, part_of)
                down = ring[slot, part_of, (quarter // 2) * half_rows:(quarter // 2 + 1) * half_rows,
                            (quarter % 2) * bcols:(quarter % 2 + 1) * bcols]
                rows_out = jnp.dot(act[e * groups * CAP:(e + 1) * groups * CAP, :], down, preferred_element_type=F32).astype(BF16)
                for b in range(groups):
                    ybuf[b, e * CAP:(e + 1) * CAP, :] = rows_out[b * CAP:(b + 1) * CAP, :]

        @pl.when(jnp.logical_and(c >= 1, c <= blocks))
        def _():
            relay_pair(c - 1)

        @pl.when(c < blocks)
        def _():
            for m in range(chips):
                for k in range(2):
                    sums = jnp.dot(terms[2 * m + k], ybuf[2 * m + k], preferred_element_type=F32)
                    part[lax.rem(c, 2), m, k] = sums[:rows] + sums[rows:2 * rows] + sums[2 * rows:]
            pair_copy(c).start()

        @pl.when(jnp.logical_and(c >= 2, c <= blocks + 1))
        def _():
            relay_first(c - 2)

        @pl.when(c >= 3)
        def _():
            finish(c - 3)
        return carry

    lax.fori_loop(0, blocks + 3, block_step, 0)
    for copy in gates + ahead + passed:
        copy.wait_send()
    for r in (1, 2):
        for k in range(2):
            across(r, k).wait_send()
    for c in range(blocks):
        for s in range(2):
            for k in range(2):
                first_copy(c, s, k).wait_send()
            second_copy(c, s).wait_send()


def moe(h2, gt, x1, wg, wu, wd, groups):
    rows, dim = h2.shape
    experts, _, ffn = wg.shape
    slots = CAP * groups
    blocks = 4
    bcols = dim // blocks
    chips = groups // 2
    dma = pltpu.SemaphoreType.DMA
    return pl.pallas_call(
        moe_kernel,
        name="moe",
        out_shape=jax.ShapeDtypeStruct((rows, dim), BF16),
        in_specs=[ANY] * 6,
        out_specs=VMEM,
        scratch_shapes=[
            pltpu.VMEM(h2.shape, BF16),
            pltpu.VMEM(gt.shape, F32),
            pltpu.VMEM(x1.shape, BF16),
            pltpu.VMEM((SLOTS, 2, dim, ffn), BF16),
            pltpu.VMEM((rows * groups, dim), BF16),
            pltpu.VMEM((experts, slots, dim), BF16),
            pltpu.VMEM((experts * slots, ffn), BF16),
            pltpu.VMEM((groups, experts * CAP, bcols), BF16),
            pltpu.VMEM((chips, 2 * experts * CAP, 2 * rows), BF16),
            pltpu.VMEM((chips, experts * CAP, 2 * rows), F32),
            pltpu.VMEM((groups, 3 * rows, experts * CAP), BF16),
            pltpu.VMEM((2, chips, 2, rows, bcols), F32),
            pltpu.VMEM((blocks, chips, rows, bcols), F32),
            pltpu.VMEM((blocks, 2, chips, rows, bcols // 2), F32),
            pltpu.VMEM((blocks, 2, 2, rows, bcols // 2), F32),
            pltpu.VMEM((blocks, 2, rows, bcols // 2), F32),
            pltpu.VMEM((groups, experts, 2 * rows), F32),
            dma((3,)), dma((SLOTS, 2)),
            dma((2, 2)), dma((2, 2)), dma((2,)), dma((2,)), dma((4, 2)), dma((4, 2)), dma((8,)), dma((8,)),
            dma((blocks,)), dma((blocks,)), dma((blocks, 2, 2)), dma((blocks, 2, 2)), dma((blocks, 2)), dma((blocks, 2)),
        ],
        compiler_params=pltpu.CompilerParams(collective_id=0, has_side_effects=True, vmem_limit_bytes=62 * 2 ** 20),
    )(h2, gt, x1, wg, wu, wd)


def solution(mesh):
    groups = mesh.shape['ep']
    batch_axes = ('dp', 'ep')

    def device_step(hidden, positions, expert_ids, k_cache, v_cache, w_query, w_key, w_value, w_out, attn_gain, q_gain, k_gain, mlp_gain, w_router, w_gate, w_up, w_down):
        ids = jnp.transpose(expert_ids, (0, 2, 1))
        router_t = w_router.T
        caches = None
        for layer in range(expert_ids.shape[0]):
            x1, h2, gt, k_new, v_new = attention(layer, positions, hidden, ids, attn_gain, q_gain, k_gain, mlp_gain, router_t,
                                                 w_query, w_key, w_value, w_out, k_cache, v_cache, caches)
            caches = (k_new, v_new)
            hidden = moe(h2, gt, x1, w_gate, w_up, w_down, groups)
        return hidden, caches[0], caches[1]

    row_spec = P(batch_axes, None)
    cache_spec = P(None, batch_axes, None, None, None)
    full_spec = P()
    expert_spec = P('ep', None, None)
    in_specs = (row_spec, P(batch_axes), P(None, batch_axes, None), cache_spec, cache_spec, full_spec, full_spec, full_spec, full_spec, full_spec, full_spec, full_spec, full_spec, full_spec, expert_spec, expert_spec, expert_spec)
    return jax.shard_map(device_step, mesh=mesh, in_specs=in_specs, out_specs=(row_spec, cache_spec, cache_spec), check_vma=False)
```

time: 181 us -> 144 us (0.80)
  Pallas kernels: 175 us -> 142 us
  other arithmetic: 3.17 us -> 0 us
    pallas_call x2, Pallas kernels: 133 us -> 103 us  [moe(): pl.pallas_call(moe_kernel, name='moe', out_shape=jax.ShapeDtypeStruct((ro...]
    pallas_call x2, Pallas kernels: 42.2 us -> 39 us  [attention(): pl.pallas_call(functools.partial(attn_kernel, layer), name='attn', out_sh...]
where the time goes in v2:
time: 144 us
  Pallas kernels  142 us (99%)
  local copies, waits for them, and re-layouts  1.67 us (1%)
    pallas_call x2, Pallas kernels, moe(): pl.pallas_call(moe_kernel, name='moe', out_shape=jax.ShapeDtypeStruct((ro...  103 us
    pallas_call x2, Pallas kernels, attention(): pl.pallas_call(functools.partial(attn_kernel, layer), name='attn', out_sh...  39 us

profile of v2, /device:TPU:0, one launch (start us, length us, event | category | flops | bytes accessed | tf_op | source)
XLA Modules:
  0.0 144.0 jit_solution(11101247843277203185)
XLA Ops:
  0.6 19.7 %attn.2 = (bf16[64,2048]{1,0:T(8,128)(2,1)}, bf16[64,2048]{1,0:T(8,128)(2,1)}, f32[64,128]{1,0:T(8,128)}, bf16[2,64,16,16,128]{4,3,2,1,0:T(8,128)(2,1)}, bf16[2,64,16,16,128]{4,3,2,1,0:T(8,128)(2,1)}) custom-call(s32[64]{0:T(128)} %pos_ref.3, bf16[64,2048]{1,0:T(8,128)(2,1)} %x_hbm.1, s32[2,8,64]{2,1,0:T(8,128)} %bitcast.4, f32[2,2048]{1,0:T(2,128)} %attn_gain_hbm.3, ...), custom_call_target="tpu_custom_call" | custom-call | tf_op jit(solution)/shard_map/attn/pallas_call | solution.py:180
  20.3 52.7 %moe.2.x_hbm = bf16[64,2048]{1,0:T(8,128)(2,1)} custom-call(bf16[64,2048]{1,0:T(8,128)(2,1)} %get-tuple-element.13.h2_hbm, f32[64,128]{1,0:T(8,128)} %get-tuple-element.14.gt_hbm, bf16[64,2048]{1,0:T(8,128)(2,1)} %get-tuple-element.15.x1_hbm, bf16[8,2048,1024]{2,1,0:T(8,128)(2,1)} %wg.3, bf16[8,2048,1024]{2,1,0:T(8,128)(2,1)} %wu.3, bf16[8,1024,2048]{2,1,0:T(8,128)(2,1)} %wd.3), custom_call_target="tpu_custom_call" | custom-call | tf_op jit(solution)/shard_map/moe/pallas_call | solution.py:500
  73.0 19.3 %attn.3 = (bf16[64,2048]{1,0:T(8,128)(2,1)}, bf16[64,2048]{1,0:T(8,128)(2,1)}, f32[64,128]{1,0:T(8,128)}, bf16[2,64,16,16,128]{4,3,2,1,0:T(8,128)(2,1)}, bf16[2,64,16,16,128]{4,3,2,1,0:T(8,128)(2,1)}) custom-call(s32[64]{0:T(128)} %pos_ref.3, bf16[64,2048]{1,0:T(8,128)(2,1)} %moe.2.x_hbm, ...), custom_call_target="tpu_custom_call", output_to_operand_aliasing={{3}: (14, {}), {4}: (15, {})} | custom-call | tf_op jit(solution)/shard_map/attn/pallas_call | solution.py:180
  92.3 49.9 %moe.3 = bf16[64,2048]{1,0:T(8,128)(2,1)} custom-call(bf16[64,2048]{1,0:T(8,128)(2,1)} %get-tuple-element.18.h2_hbm, f32[64,128]{1,0:T(8,128)} %get-tuple-element.19.gt_hbm, bf16[64,2048]{1,0:T(8,128)(2,1)} %get-tuple-element.20.x1_hbm, bf16[8,2048,1024]{2,1,0:T(8,128)(2,1)} %wg.3, bf16[8,2048,1024]{2,1,0:T(8,128)(2,1)} %wu.3, bf16[8,1024,2048]{2,1,0:T(8,128)(2,1)} %wd.3), custom_call_target="tpu_custom_call" | custom-call | tf_op jit(solution)/shard_map/moe/pallas_call | solution.py:500
  142.3 1.7 %copy.25 = bf16[64,2048]{1,0:T(8,128)(2,1)} copy(bf16[64,2048]{1,0:T(8,128)(2,1)} %moe.3) | data formatting | bytes 524288

commit v3 on v2

--- a/solution.py
+++ b/solution.py
@@ -11,8 +11,11 @@
 RMS_EPS = 1e-5
 ROPE_BASE = 10000.0
 CAP = 16
-SLOTS = 5
+SLOTS = 6
 FCOLS = 512
+ACOLS = 512
+MID = 4
+LAG = 7
 F32 = jnp.float32
 BF16 = jnp.bfloat16
 ANY = pl.BlockSpec(memory_space=pl.ANY)
@@ -27,18 +30,17 @@
     return values * inv_rms * gain_row
 
 
-def attn_kernel(layer, pos_ref, x_hbm, ids_hbm, attn_gain_hbm, q_gain_hbm, k_gain_hbm, mlp_gain_hbm, router_hbm,
+def attn_kernel(layer, pos_hbm, x_hbm, attn_gain_hbm, q_gain_hbm, k_gain_hbm,
                 wq, wk, wv, wo, k_in, v_in, *rest):
     if layer > 0:
         rest = rest[2:]
-    (x1_ref, h2_ref, gt_ref, k_out, v_out,
-     x_ref, ids_ref, attn_gain, q_gain, k_gain, mlp_gain, router_ref, angle,
+    (x1_ref, k_out, v_out,
+     pos_ref, x_ref, attn_gain, q_gain, k_gain, angle,
      wbuf, kbuf, vbuf, h_buf, lin, q2d, k2d, probs, mixed, ssem, wsem, csem, osem) = rest
     rows, dim = x_ref.shape
     heads, hd = k_in.shape[3], k_in.shape[4]
     cache_len = k_in.shape[2]
     half = dim // 2
-    experts = router_ref.shape[0]
 
     def wcopy(i):
         src = (wq, wk, wv, wo)[i // 2]
@@ -47,8 +49,7 @@
     kcopy = pltpu.make_async_copy(k_in.at[layer], kbuf, csem.at[0])
     vcopy = pltpu.make_async_copy(v_in.at[layer], vbuf, csem.at[1])
     small = [pltpu.make_async_copy(src, dst, ssem.at[n]) for n, (src, dst) in enumerate((
-        (x_hbm, x_ref), (attn_gain_hbm, attn_gain), (ids_hbm, ids_ref), (q_gain_hbm, q_gain), (k_gain_hbm, k_gain),
-        (mlp_gain_hbm, mlp_gain), (router_hbm, router_ref)))]
+        (x_hbm, x_ref), (attn_gain_hbm, attn_gain), (pos_hbm, pos_ref), (q_gain_hbm, q_gain), (k_gain_hbm, k_gain)))]
     for copy in small:
         copy.start()
     for i in range(4):
@@ -66,19 +67,14 @@
     angles = angle[...]
     cos = jnp.cos(angles)
     sin = jnp.where(lane < hd // 2, -1.0, 1.0) * jnp.sin(angles)
-    expert_row = lax.broadcasted_iota(jnp.int32, (experts, 128), 0)
-    wide_ids = jnp.concatenate([ids_ref[layer]] * (128 // rows), axis=1)
-    hits = expert_row == wide_ids[0:1, :]
-    for j in range(1, wide_ids.shape[0]):
-        hits = jnp.logical_or(hits, expert_row == wide_ids[j:j + 1, :])
-    member = jnp.where(hits, 1.0, 0.0)
-
     def project(which):
         for j in range(2):
             wcopy(2 * which + j).wait()
             for copy in after.get(2 * which + j, ()):
                 copy.start(priority=1)
-            lin[:, j * half:(j + 1) * half] = jnp.dot(h_buf[...], wbuf[2 * which + j], preferred_element_type=F32)
+            for n in range(0, half, ACOLS):
+                lin[:, j * half + n:j * half + n + ACOLS] = jnp.dot(
+                    h_buf[...], wbuf[2 * which + j, :, n:n + ACOLS], preferred_element_type=F32)
 
     def spread(gain_ref, dst):
         values = lin[...]
@@ -158,23 +154,16 @@
         cols = slice(j * half, (j + 1) * half)
         wcopy(6 + j).wait()
         lin[:, cols] = x_ref[:, cols].astype(F32) + jnp.dot(mixed[...], wbuf[6 + j], preferred_element_type=F32)
-    x1 = lin[...].astype(BF16)
-    x1_ref[...] = x1
-    h2 = rms_rows(x1.astype(F32), mlp_gain[layer:layer + 1, :]).astype(BF16)
-    h2_ref[...] = h2
-    logits = lax.dot_general(router_ref[...], jnp.concatenate([h2] * (128 // rows), axis=0), NT, preferred_element_type=F32)
-    logits = jnp.exp(logits - jnp.max(logits, axis=0, keepdims=True))
-    router_probs = logits / jnp.sum(logits, axis=0, keepdims=True)
-    gt_ref[...] = jnp.where(member > 0.5, router_probs, -1.0)
+    x1_ref[...] = lin[...].astype(BF16)
     for g in range(groups):
         for which in range(2):
             out_copy(which, g).wait()
 
 
-def attention(layer, pos, x, ids, attn_gain, q_gain, k_gain, mlp_gain, router_t, wq, wk, wv, wo, k_in, v_in, prev):
+def attention(layer, pos, x, attn_gain, q_gain, k_gain, wq, wk, wv, wo, k_in, v_in, prev):
     rows, dim = x.shape
     _, _, cache_len, heads, hd = k_in.shape
-    aliases = {} if prev is None else {14: 3, 15: 4}
+    aliases = {} if prev is None else {11: 1, 12: 2}
     prev = () if prev is None else prev
     groups = rows // 8
     return pl.pallas_call(
@@ -182,15 +171,14 @@
         name="attn",
         out_shape=(
             jax.ShapeDtypeStruct((rows, dim), BF16),
-            jax.ShapeDtypeStruct((rows, dim), BF16),
-            jax.ShapeDtypeStruct((router_t.shape[0], 128), F32),
             jax.ShapeDtypeStruct(k_in.shape, BF16),
             jax.ShapeDtypeStruct(v_in.shape, BF16),
         ),
-        in_specs=[SMEM] + [ANY] * (13 + len(prev)),
-        out_specs=(VMEM, VMEM, VMEM, ANY, ANY),
+        in_specs=[ANY] * (11 + len(prev)),
+        out_specs=(VMEM, ANY, ANY),
         scratch_shapes=[
-            *[pltpu.VMEM(a.shape, a.dtype) for a in (x, ids, attn_gain, q_gain, k_gain, mlp_gain, router_t)],
+            pltpu.SMEM(pos.shape, pos.dtype),
+            *[pltpu.VMEM(a.shape, a.dtype) for a in (x, attn_gain, q_gain, k_gain)],
             pltpu.VMEM((rows, hd), F32),
             pltpu.VMEM((8, dim, dim // 2), BF16),
             pltpu.VMEM(k_in.shape[1:], BF16),
@@ -201,27 +189,30 @@
             pltpu.VMEM((rows * heads, hd), F32),
             pltpu.VMEM((rows * heads, cache_len * heads), BF16),
             pltpu.VMEM((rows, dim), BF16),
-            pltpu.SemaphoreType.DMA((7,)),
+            pltpu.SemaphoreType.DMA((5,)),
             pltpu.SemaphoreType.DMA((8,)),
             pltpu.SemaphoreType.DMA((2,)),
             pltpu.SemaphoreType.DMA((2, groups)),
         ],
         input_output_aliases=aliases,
         compiler_params=pltpu.CompilerParams(vmem_limit_bytes=60 * 2 ** 20),
-    )(pos, x, ids, attn_gain, q_gain, k_gain, mlp_gain, router_t, wq, wk, wv, wo, k_in, v_in, *prev)
-
-
-def moe_kernel(h2_hbm, gt_hbm, x1_hbm, wg, wu, wd, out_ref,
-               h2_ref, gt_ref, x1_ref, ring, xall, xs, act, ybuf, pick, spread, terms, part, dr, sbuf, step1, step2, gtall,
+    )(pos, x, attn_gain, q_gain, k_gain, wq, wk, wv, wo, k_in, v_in, *prev)
+
+
+def moe_kernel(layer, x1_hbm, mlp_gain_hbm, ids_hbm, router_hbm, wg, wu, wd, out_ref,
+               x1_ref, mlp_gain, ids_ref, router_ref, gt_ref, ring, xall, xs, ybuf, pick, terms, part, dr, step1, step2, gtall,
                ssem, wsem, a_send, a_recv, f_send, f_recv, d_send, d_recv, g_send, g_recv, p_send, p_recv, u_send, u_recv, w_send, w_recv):
-    rows, dim = h2_ref.shape
+    rows, dim = x1_ref.shape
     experts, _, ffn = wg.shape
+    all_experts = router_ref.shape[0]
     groups = xs.shape[1] // CAP
     chips = groups // 2
     bcols = ybuf.shape[2]
     blocks = dim // bcols
     sub = bcols // 2
-    pairs = experts + blocks
+    wcols = ring.shape[3] // 2
+    per = wcols // bcols
+    pairs = experts + dim // wcols
     half_rows = ring.shape[2] // 2
     hrows = rows // 2
 
@@ -230,19 +221,19 @@
         pltpu.make_async_copy(wu.at[i], ring.at[slot, 1], wsem.at[slot, 1]).start(priority=1)
 
     def start_down(c, slot):
-        cols = pl.ds(pl.multiple_of(c * bcols, bcols), bcols)
+        cols = pl.ds(pl.multiple_of(c * wcols, wcols), wcols)
         for e in range(experts):
             part_of, quarter = e // 4, e % 4
             pltpu.make_async_copy(
                 wd.at[e, :, cols],
-                ring.at[slot, part_of, pl.ds((quarter // 2) * half_rows, half_rows), pl.ds((quarter % 2) * bcols, bcols)],
+                ring.at[slot, part_of, pl.ds((quarter // 2) * half_rows, half_rows), pl.ds((quarter % 2) * wcols, wcols)],
                 wsem.at[slot, part_of]).start(priority=1)
 
     def wait_weights(slot, part_of):
         pltpu.make_async_copy(wg.at[0], ring.at[slot, part_of], wsem.at[slot, part_of]).wait()
 
     small = [pltpu.make_async_copy(src, dst, ssem.at[n]) for n, (src, dst) in enumerate((
-        (h2_hbm, h2_ref), (gt_hbm, gt_ref), (x1_hbm, x1_ref)))]
+        (x1_hbm, x1_ref), (mlp_gain_hbm, mlp_gain), (ids_hbm, ids_ref), (router_hbm, router_ref)))]
     for copy in small:
         copy.start()
     for i in range(SLOTS):
@@ -267,6 +258,18 @@
         pl.semaphore_signal(barrier, inc=1, device_id={"ep": device_at(q)}, device_id_type=MESH)
     for copy in small:
         copy.wait()
+    h2 = rms_rows(x1_ref[...].astype(F32), mlp_gain[layer:layer + 1, :]).astype(BF16)
+    xall[pl.ds(pl.multiple_of(me * rows, rows), rows), :] = h2
+    expert_row = lax.broadcasted_iota(jnp.int32, (all_experts, 128), 0)
+    wide_ids = jnp.concatenate([ids_ref[layer]] * (128 // rows), axis=1)
+    hits = expert_row == wide_ids[0:1, :]
+    for j in range(1, wide_ids.shape[0]):
+        hits = jnp.logical_or(hits, expert_row == wide_ids[j:j + 1, :])
+    member = jnp.where(hits, 1.0, 0.0)
+    logits = lax.dot_general(router_ref[...], jnp.concatenate([h2] * (128 // rows), axis=0), NT, preferred_element_type=F32)
+    logits = jnp.exp(logits - jnp.max(logits, axis=0, keepdims=True))
+    router_probs = logits / jnp.sum(logits, axis=0, keepdims=True)
+    gt_ref[...] = jnp.where(member > 0.5, router_probs, -1.0)
     pl.semaphore_wait(barrier, 7)
 
     def rows_of(dev):
@@ -287,16 +290,15 @@
              for q in range(1, 8)]
 
     def across(r, k):
-        return remote(h2_ref.at[pl.ds(k * hrows, hrows)], xall.at[half_of(me, k)], a_send.at[r - 1, k], a_recv.at[r - 1, k],
+        return remote(xall.at[half_of(me, k)], xall.at[half_of(me, k)], a_send.at[r - 1, k], a_recv.at[r - 1, k],
                       device_at(2 * r))
 
-    own = remote(h2_ref, xall.at[rows_of(me)], d_send.at[0, 0], d_recv.at[0, 0], partner)
+    own = remote(xall.at[rows_of(me)], xall.at[rows_of(me)], d_send.at[0, 0], d_recv.at[0, 0], partner)
     for copy in gates:
         copy.start()
     for r, k in ((1, 0), (2, 1), (1, 1), (2, 0)):
         across(r, k).start()
     own.start()
-    xall[rows_of(me), :] = h2_ref[...]
     gtall[me] = gt_ref[experts_of(me), :]
     for copy in gates:
         copy.wait_recv()
@@ -321,9 +323,9 @@
             pick[j, at, :] = jnp.where(jnp.logical_and(hit, left), 1.0, 0.0).astype(BF16)
             pick[j, width + e * CAP:width + (e + 1) * CAP, :] = jnp.where(
                 jnp.logical_and(hit, jnp.logical_not(left)), 1.0, 0.0).astype(BF16)
-            spread[j, at, :] = jnp.where(hit, gate_rows[line, :], 0.0)
+            part[0, 0, e * CAP // rows, j, e * CAP % rows:e * CAP % rows + CAP, :] = jnp.where(hit, gate_rows[line, :], 0.0)
     for j in range(chips):
-        gated = jnp.transpose(spread[j])
+        gated = jnp.transpose(jnp.concatenate([part[0, 0, 0, j], part[0, 0, 1, j]], axis=0))
         high = gated.astype(BF16)
         rest = gated - high.astype(F32)
         middle = rest.astype(BF16)
@@ -359,7 +361,7 @@
                               preferred_element_type=F32).astype(BF16)
         for k in range(2):
             for e in range(experts):
-                xs[e, pl.ds(pl.multiple_of((2 * j + k) * CAP, CAP), CAP), :] = chosen_rows[k * width + e * CAP:k * width + (e + 1) * CAP, :]
+                xs[e + 1, pl.ds(pl.multiple_of((2 * j + k) * CAP, CAP), CAP), :] = chosen_rows[k * width + e * CAP:k * width + (e + 1) * CAP, :]
 
     own.wait_recv()
     take_rows(0)
@@ -382,14 +384,13 @@
 
     def expert_step(e, carry):
         slot = lax.rem(e, SLOTS)
-        at = pl.ds(pl.multiple_of(e * groups * CAP, groups * CAP), groups * CAP)
         wait_weights(slot, 0)
         wait_weights(slot, 1)
         for n in range(ffn // FCOLS):
             cols = slice(n * FCOLS, (n + 1) * FCOLS)
-            gate_act = jnp.dot(xs[e], ring[slot, 0, :, cols], preferred_element_type=F32)
-            up_act = jnp.dot(xs[e], ring[slot, 1, :, cols], preferred_element_type=F32)
-            act[at, cols] = (jax.nn.silu(gate_act) * up_act).astype(BF16)
+            gate_act = jnp.dot(xs[e + 1], ring[slot, 0, :, cols], preferred_element_type=F32)
+            up_act = jnp.dot(xs[e + 1], ring[slot, 1, :, cols], preferred_element_type=F32)
+            xs[e, :, cols] = (jax.nn.silu(gate_act) * up_act).astype(BF16)
 
         @pl.when(e + SLOTS < experts)
         def _():
@@ -403,24 +404,22 @@
     lax.fori_loop(0, experts, expert_step, 0)
 
     def pair_copy(c):
-        return remote(part.at[lax.rem(c, 2), :, 1 - core], dr.at[c], p_send.at[c], p_recv.at[c], partner)
+        return remote(part.at[lax.rem(c, 2), 1 - core], dr.at[c], p_send.at[c], p_recv.at[c], partner)
 
     def first_copy(c, s, k):
         to = 1 + s
-        return remote(sbuf.at[c, s, chip_at((to, 3)[k])], step1.at[c, s, k], u_send.at[c, s, k], u_recv.at[c, s, k],
+        return remote(dr.at[c, s, chip_at((to, 3)[k])], step1.at[c, s, k], u_send.at[c, s, k], u_recv.at[c, s, k],
                       device_at(2 * to))
 
     def second_copy(c, s):
         to = 2 - s
-        return remote(sbuf.at[c, s, chip_at(to)], step2.at[c, s], w_send.at[c, s], w_recv.at[c, s], device_at(2 * to))
+        return remote(dr.at[c, s, chip_at(to)], step2.at[c, s], w_send.at[c, s], w_recv.at[c, s], device_at(2 * to))
 
     def relay_pair(c):
         copy = pair_copy(c)
         copy.wait_send()
         copy.wait_recv()
-        both = part[lax.rem(c, 2), :, core] + dr[c]
-        for s in range(2):
-            sbuf[c, s] = both[:, :, s * sub:(s + 1) * sub]
+        dr[c] = dr[c] + part[lax.rem(c, 2), core]
         for k in (1, 0):
             for s in range(2):
                 first_copy(c, s, k).start()
@@ -429,7 +428,7 @@
         for s in range(2):
             first_copy(c, s, 1).wait_recv()
             to = chip_at(2 - s)
-            sbuf[c, s, to] = sbuf[c, s, to] + step1[c, s, 1]
+            dr[c, s, to] = dr[c, s, to] + step1[c, s, 1]
             second_copy(c, s).start()
 
     def finish(c):
@@ -437,21 +436,24 @@
             first_copy(c, s, 0).wait_recv()
             second_copy(c, s).wait_recv()
             cols = pl.ds(pl.multiple_of(c * bcols + s * sub, sub), sub)
-            total = sbuf[c, s, chip] + step1[c, s, 0] + step2[c, s]
-            out_ref[:, cols] = (x1_ref[:, cols].astype(F32) + total).astype(BF16)
+            total = dr[c, s, chip] + step1[c, s, 0] + step2[c, s]
+            out_ref[:, cols] = (x1_ref[:, cols].astype(F32) + total).astype(out_ref.dtype)
 
     def block_step(c, carry):
-        slot = lax.rem(experts + c, SLOTS)
+        slot = lax.rem(experts + lax.div(c, per), SLOTS)
+        shift = lax.rem(c, per) * bcols
 
         @pl.when(c < blocks)
         def _():
             for e in range(experts):
                 part_of, quarter = e // 4, e % 4
                 if quarter == 0:
-                    wait_weights(slot, part_of)
+                    @pl.when(shift == 0)
+                    def _():
+                        wait_weights(slot, part_of)
                 down = ring[slot, part_of, (quarter // 2) * half_rows:(quarter // 2 + 1) * half_rows,
-                            (quarter % 2) * bcols:(quarter % 2 + 1) * bcols]
-                rows_out = jnp.dot(act[e * groups * CAP:(e + 1) * groups * CAP, :], down, preferred_element_type=F32).astype(BF16)
+                            pl.ds(pl.multiple_of((quarter % 2) * wcols + shift, bcols), bcols)]
+                rows_out = jnp.dot(xs[e, :, :ffn], down, preferred_element_type=F32).astype(BF16)
                 for b in range(groups):
                     ybuf[b, e * CAP:(e + 1) * CAP, :] = rows_out[b * CAP:(b + 1) * CAP, :]
 
@@ -464,19 +466,21 @@
             for m in range(chips):
                 for k in range(2):
                     sums = jnp.dot(terms[2 * m + k], ybuf[2 * m + k], preferred_element_type=F32)
-                    part[lax.rem(c, 2), m, k] = sums[:rows] + sums[rows:2 * rows] + sums[2 * rows:]
+                    sums = sums[:rows] + sums[rows:2 * rows] + sums[2 * rows:]
+                    for s in range(2):
+                        part[lax.rem(c, 2), k, s, m] = sums[:, s * sub:(s + 1) * sub]
             pair_copy(c).start()
 
-        @pl.when(jnp.logical_and(c >= 2, c <= blocks + 1))
-        def _():
-            relay_first(c - 2)
-
-        @pl.when(c >= 3)
-        def _():
-            finish(c - 3)
+        @pl.when(jnp.logical_and(c >= MID, c < blocks + MID))
+        def _():
+            relay_first(c - MID)
+
+        @pl.when(c >= LAG)
+        def _():
+            finish(c - LAG)
         return carry
 
-    lax.fori_loop(0, blocks + 3, block_step, 0)
+    lax.fori_loop(0, blocks + LAG, block_step, 0)
     for copy in gates + ahead + passed:
         copy.wait_send()
     for r in (1, 2):
@@ -489,44 +493,40 @@
             second_copy(c, s).wait_send()
 
 
-def moe(h2, gt, x1, wg, wu, wd, groups):
-    rows, dim = h2.shape
+def moe(layer, x1, mlp_gain, ids, router_t, wg, wu, wd, groups, out_type):
+    rows, dim = x1.shape
     experts, _, ffn = wg.shape
     slots = CAP * groups
-    blocks = 4
+    blocks = 8
     bcols = dim // blocks
     chips = groups // 2
     dma = pltpu.SemaphoreType.DMA
     return pl.pallas_call(
-        moe_kernel,
+        functools.partial(moe_kernel, layer),
         name="moe",
-        out_shape=jax.ShapeDtypeStruct((rows, dim), BF16),
-        in_specs=[ANY] * 6,
+        out_shape=jax.ShapeDtypeStruct((rows, dim), out_type),
+        in_specs=[ANY] * 7,
         out_specs=VMEM,
         scratch_shapes=[
-            pltpu.VMEM(h2.shape, BF16),
-            pltpu.VMEM(gt.shape, F32),
-            pltpu.VMEM(x1.shape, BF16),
+            *[pltpu.VMEM(a.shape, a.dtype) for a in (x1, mlp_gain, ids, router_t)],
+            pltpu.VMEM((router_t.shape[0], 128), F32),
             pltpu.VMEM((SLOTS, 2, dim, ffn), BF16),
             pltpu.VMEM((rows * groups, dim), BF16),
-            pltpu.VMEM((experts, slots, dim), BF16),
-            pltpu.VMEM((experts * slots, ffn), BF16),
+            pltpu.VMEM((experts + 1, slots, dim), BF16),
             pltpu.VMEM((groups, experts * CAP, bcols), BF16),
             pltpu.VMEM((chips, 2 * experts * CAP, 2 * rows), BF16),
-            pltpu.VMEM((chips, experts * CAP, 2 * rows), F32),
             pltpu.VMEM((groups, 3 * rows, experts * CAP), BF16),
-            pltpu.VMEM((2, chips, 2, rows, bcols), F32),
-            pltpu.VMEM((blocks, chips, rows, bcols), F32),
+            pltpu.VMEM((2, 2, 2, chips, rows, bcols // 2), F32),
             pltpu.VMEM((blocks, 2, chips, rows, bcols // 2), F32),
             pltpu.VMEM((blocks, 2, 2, rows, bcols // 2), F32),
             pltpu.VMEM((blocks, 2, rows, bcols // 2), F32),
             pltpu.VMEM((groups, experts, 2 * rows), F32),
-            dma((3,)), dma((SLOTS, 2)),
+            dma((4,)), dma((SLOTS, 2)),
             dma((2, 2)), dma((2, 2)), dma((2,)), dma((2,)), dma((4, 2)), dma((4, 2)), dma((8,)), dma((8,)),
             dma((blocks,)), dma((blocks,)), dma((blocks, 2, 2)), dma((blocks, 2, 2)), dma((blocks, 2)), dma((blocks, 2)),
         ],
-        compiler_params=pltpu.CompilerParams(collective_id=0, has_side_effects=True, vmem_limit_bytes=62 * 2 ** 20),
-    )(h2, gt, x1, wg, wu, wd)
+        compiler_params=pltpu.CompilerParams(collective_id=layer, has_side_effects=True, vmem_limit_bytes=67043328),
+    )(x1, mlp_gain, ids, router_t, wg, wu, wd)
 
 
 def solution(mesh):
@@ -538,11 +538,12 @@
         router_t = w_router.T
         caches = None
         for layer in range(expert_ids.shape[0]):
-            x1, h2, gt, k_new, v_new = attention(layer, positions, hidden, ids, attn_gain, q_gain, k_gain, mlp_gain, router_t,
-                                                 w_query, w_key, w_value, w_out, k_cache, v_cache, caches)
+            x1, k_new, v_new = attention(layer, positions, hidden, attn_gain, q_gain, k_gain,
+                                         w_query, w_key, w_value, w_out, k_cache, v_cache, caches)
             caches = (k_new, v_new)
-            hidden = moe(h2, gt, x1, w_gate, w_up, w_down, groups)
-        return hidden, caches[0], caches[1]
+            out_type = BF16
+            hidden = moe(layer, x1, mlp_gain, ids, router_t, w_gate, w_up, w_down, groups, out_type)
+        return hidden.astype(BF16), caches[0], caches[1]
 
     row_spec = P(batch_axes, None)
     cache_spec = P(None, batch_axes, None, None, None)

time: 144 us -> 140 us (0.972)
  Pallas kernels: 142 us -> 137 us
    pallas_call x2, Pallas kernels: 39 us -> 35.9 us  [attention(): pl.pallas_call(functools.partial(attn_kernel, layer), name='attn', out_sh...]
where the time goes in v3:
time: 140 us
  Pallas kernels  137 us (98%)
  local copies, waits for them, and re-layouts  1.67 us (1%)
    pallas_call x2, Pallas kernels, moe(): pl.pallas_call(functools.partial(moe_kernel, layer), name='moe', out_shap...  101 us
    pallas_call x2, Pallas kernels, attention(): pl.pallas_call(functools.partial(attn_kernel, layer), name='attn', out_sh...  35.9 us

profile of v3, /device:TPU:0, one launch (start us, length us, event | category | flops | bytes accessed | tf_op | source)
XLA Modules:
  0.0 139.6 jit_solution(17979115139912279262)
XLA Ops:
  0.6 18.2 %attn.2 = (bf16[64,2048]{1,0:T(8,128)(2,1)}, bf16[2,64,16,16,128]{4,3,2,1,0:T(8,128)(2,1)}, bf16[2,64,16,16,128]{4,3,2,1,0:T(8,128)(2,1)}) custom-call(s32[64]{0:T(128)} %pos_hbm.3, bf16[64,2048]{1,0:T(8,128)(2,1)} %x_hbm.1, f32[2,2048]{1,0:T(2,128)} %attn_gain_hbm.3, f32[2,2048]{1,0:T(2,128)} %q_gain_hbm.3, f32[2,2048]{1,0:T(2,128)} %k_gain_hbm.3, ...), custom_call_target="tpu_custom_call" | custom-call | tf_op jit(solution)/shard_map/attn/pallas_call | solution.py:169
  18.8 52.0 %moe.2.x_hbm = bf16[64,2048]{1,0:T(8,128)(2,1)} custom-call(bf16[64,2048]{1,0:T(8,128)(2,1)} %get-tuple-element.9.x1_hbm, f32[2,2048]{1,0:T(2,128)} %mlp_gain_hbm.3, s32[2,8,64]{2,1,0:T(8,128)} %bitcast.4, bf16[64,2048]{1,0:T(8,128)(2,1)} %bitcast.2, bf16[8,2048,1024]{2,1,0:T(8,128)(2,1)} %wg.3, bf16[8,2048,1024]{2,1,0:T(8,128)(2,1)} %wu.3, ...), custom_call_target="tpu_custom_call" | custom-call | tf_op jit(solution)/shard_map/moe/pallas_call | solution.py:504
  70.9 17.7 %attn.3 = (bf16[64,2048]{1,0:T(8,128)(2,1)}, bf16[2,64,16,16,128]{4,3,2,1,0:T(8,128)(2,1)}, bf16[2,64,16,16,128]{4,3,2,1,0:T(8,128)(2,1)}) custom-call(s32[64]{0:T(128)} %pos_hbm.3, bf16[64,2048]{1,0:T(8,128)(2,1)} %moe.2.x_hbm, f32[2,2048]{1,0:T(2,128)} %attn_gain_hbm.3, f32[2,2048]{1,0:T(2,128)} %q_gain_hbm.3, ...), custom_call_target="tpu_custom_call", output_to_operand_aliasing={{1}: (11, {}), {2}: (12, {})} | custom-call | tf_op jit(solution)/shard_map/attn/pallas_call | solution.py:169
  88.6 49.3 %moe.3 = bf16[64,2048]{1,0:T(8,128)(2,1)} custom-call(bf16[64,2048]{1,0:T(8,128)(2,1)} %get-tuple-element.12.x1_hbm, f32[2,2048]{1,0:T(2,128)} %mlp_gain_hbm.3, s32[2,8,64]{2,1,0:T(8,128)} %bitcast.5, bf16[64,2048]{1,0:T(8,128)(2,1)} %bitcast.3, bf16[8,2048,1024]{2,1,0:T(8,128)(2,1)} %wg.3, bf16[8,2048,1024]{2,1,0:T(8,128)(2,1)} %wu.3, bf16[8,1024,2048]{2,1,0:T(8,128)(2,1)} %wd.3), custom_call_target="tpu_custom_call" | custom-call | tf_op jit(solution)/shard_map/moe/pallas_call | solution.py:504
  137.9 1.7 %copy.25 = bf16[64,2048]{1,0:T(8,128)(2,1)} copy(bf16[64,2048]{1,0:T(8,128)(2,1)} %moe.3) | data formatting | bytes 524288

commit v4 on v3

--- a/solution.py
+++ b/solution.py
@@ -30,43 +30,56 @@
     return values * inv_rms * gain_row
 
 
-def attn_kernel(layer, pos_hbm, x_hbm, attn_gain_hbm, q_gain_hbm, k_gain_hbm,
-                wq, wk, wv, wo, k_in, v_in, *rest):
-    if layer > 0:
-        rest = rest[2:]
-    (x1_ref, k_out, v_out,
-     pos_ref, x_ref, attn_gain, q_gain, k_gain, angle,
-     wbuf, kbuf, vbuf, h_buf, lin, q2d, k2d, probs, mixed, ssem, wsem, csem, osem) = rest
-    rows, dim = x_ref.shape
-    heads, hd = k_in.shape[3], k_in.shape[4]
-    cache_len = k_in.shape[2]
-    half = dim // 2
-
-    def wcopy(i):
-        src = (wq, wk, wv, wo)[i // 2]
-        return pltpu.make_async_copy(src.at[layer, :, pl.ds((i % 2) * half, half)], wbuf.at[i], wsem.at[i])
-
-    kcopy = pltpu.make_async_copy(k_in.at[layer], kbuf, csem.at[0])
-    vcopy = pltpu.make_async_copy(v_in.at[layer], vbuf, csem.at[1])
-    small = [pltpu.make_async_copy(src, dst, ssem.at[n]) for n, (src, dst) in enumerate((
-        (x_hbm, x_ref), (attn_gain_hbm, attn_gain), (pos_hbm, pos_ref), (q_gain_hbm, q_gain), (k_gain_hbm, k_gain)))]
-    for copy in small:
-        copy.start()
-    for i in range(4):
-        wcopy(i).start(priority=1)
-    after = {0: [kcopy], 1: [wcopy(4)], 2: [wcopy(5)], 3: [vcopy], 4: [wcopy(6)], 5: [wcopy(7)]}
-    for copy in small:
-        copy.wait()
-    x = x_ref[...].astype(F32)
-    h_buf[...] = rms_rows(x, attn_gain[layer:layer + 1, :]).astype(BF16)
+def rotary(angle, pos_ref, rows, hd):
     lane = lax.broadcasted_iota(jnp.int32, (1, hd), 1)
     exponent = (lane % (hd // 2)).astype(F32) / (hd // 2)
     frequencies = jnp.exp(exponent * -math.log(ROPE_BASE))
     for b in range(rows):
         angle[b:b + 1, :] = frequencies * pos_ref[b].astype(F32)
     angles = angle[...]
-    cos = jnp.cos(angles)
-    sin = jnp.where(lane < hd // 2, -1.0, 1.0) * jnp.sin(angles)
+    return jnp.cos(angles), jnp.where(lane < hd // 2, -1.0, 1.0) * jnp.sin(angles)
+
+
+def attn_kernel(layer, ready, pos_hbm, x_hbm, attn_gain_hbm, q_gain_hbm, k_gain_hbm,
+                wq, wk, wv, wo, k_in, v_in, *rest):
+    if layer > 0:
+        rest = rest[2:]
+    if ready:
+        qkv_hbm, *rest = rest
+    (x1_ref, k_out, v_out,
+     qkv, pos_ref, x_ref, attn_gain, q_gain, k_gain, angle,
+     wbuf, kbuf, vbuf, h_buf, lin, q2d, k2d, probs, mixed, ssem, wsem, csem, osem) = rest
+    rows, dim = x_ref.shape
+    heads, hd = k_in.shape[3], k_in.shape[4]
+    cache_len = k_in.shape[2]
+    half = dim // 2
+
+    def wcopy(i):
+        src = (wq, wk, wv, wo)[i // 2]
+        return pltpu.make_async_copy(src.at[layer, :, pl.ds((i % 2) * half, half)], wbuf.at[i], wsem.at[i])
+
+    kcopy = pltpu.make_async_copy(k_in.at[layer], kbuf, csem.at[0])
+    vcopy = pltpu.make_async_copy(v_in.at[layer], vbuf, csem.at[1])
+    small = [pltpu.make_async_copy(src, dst, ssem.at[n]) for n, (src, dst) in enumerate((
+        (x_hbm, x_ref), (pos_hbm, pos_ref), *([(qkv_hbm, qkv)] if ready else [
+            (attn_gain_hbm, attn_gain), (q_gain_hbm, q_gain), (k_gain_hbm, k_gain)])))]
+    for copy in small:
+        copy.start()
+    if ready:
+        kcopy.start()
+        for copy in (vcopy, wcopy(6), wcopy(7)):
+            copy.start(priority=1)
+    else:
+        for i in range(4):
+            wcopy(i).start(priority=1)
+    after = {} if ready else {0: [kcopy], 1: [wcopy(4)], 2: [wcopy(5)], 3: [vcopy], 4: [wcopy(6)], 5: [wcopy(7)]}
+    for copy in small:
+        copy.wait()
+    if not ready:
+        x = x_ref[...].astype(F32)
+        h_buf[...] = rms_rows(x, attn_gain[layer:layer + 1, :]).astype(BF16)
+    cos, sin = (None, None) if ready else rotary(angle, pos_ref, rows, hd)
+
     def project(which):
         for j in range(2):
             wcopy(2 * which + j).wait()
@@ -85,10 +98,18 @@
             part = part * cos + pltpu.roll(part, hd // 2, 1) * sin
             dst[pl.ds(h, rows, stride=heads), :] = part
 
-    project(0)
-    spread(q_gain, q2d)
-    project(1)
-    spread(k_gain, k2d)
+    def arrange(which, dst):
+        for h in range(heads):
+            dst[pl.ds(h, rows, stride=heads), :] = qkv[which, :, h * hd:(h + 1) * hd].astype(F32)
+
+    if ready:
+        arrange(0, q2d)
+        arrange(1, k2d)
+    else:
+        project(0)
+        spread(q_gain, q2d)
+        project(1)
+        spread(k_gain, k2d)
     kcopy.wait()
 
     span = cache_len * heads
@@ -127,12 +148,15 @@
         return carry
 
     lax.fori_loop(0, groups, score, 0)
-    project(2)
-    out_copy(0, groups - 1).start()
     v2d = q2d
     o2d = k2d
-    for h in range(heads):
-        v2d[pl.ds(h, rows, stride=heads), :] = lin[:, h * hd:(h + 1) * hd]
+    if ready:
+        arrange(2, v2d)
+    else:
+        project(2)
+        for h in range(heads):
+            v2d[pl.ds(h, rows, stride=heads), :] = lin[:, h * hd:(h + 1) * hd]
+    out_copy(0, groups - 1).start()
     vcopy.wait()
 
     def mix(g, carry):
@@ -160,23 +184,24 @@
             out_copy(which, g).wait()
 
 
-def attention(layer, pos, x, attn_gain, q_gain, k_gain, wq, wk, wv, wo, k_in, v_in, prev):
+def attention(layer, pos, x, attn_gain, q_gain, k_gain, wq, wk, wv, wo, k_in, v_in, prev, ready):
     rows, dim = x.shape
     _, _, cache_len, heads, hd = k_in.shape
     aliases = {} if prev is None else {11: 1, 12: 2}
     prev = () if prev is None else prev
     groups = rows // 8
     return pl.pallas_call(
-        functools.partial(attn_kernel, layer),
+        functools.partial(attn_kernel, layer, bool(ready)),
         name="attn",
         out_shape=(
             jax.ShapeDtypeStruct((rows, dim), BF16),
             jax.ShapeDtypeStruct(k_in.shape, BF16),
             jax.ShapeDtypeStruct(v_in.shape, BF16),
         ),
-        in_specs=[ANY] * (11 + len(prev)),
+        in_specs=[ANY] * (11 + len(prev) + len(ready)),
         out_specs=(VMEM, ANY, ANY),
         scratch_shapes=[
+            pltpu.VMEM((3, rows, dim), BF16),
             pltpu.SMEM(pos.shape, pos.dtype),
             *[pltpu.VMEM(a.shape, a.dtype) for a in (x, attn_gain, q_gain, k_gain)],
             pltpu.VMEM((rows, hd), F32),
@@ -196,12 +221,17 @@
         ],
         input_output_aliases=aliases,
         compiler_params=pltpu.CompilerParams(vmem_limit_bytes=60 * 2 ** 20),
-    )(pos, x, attn_gain, q_gain, k_gain, wq, wk, wv, wo, k_in, v_in, *prev)
-
-
-def moe_kernel(layer, x1_hbm, mlp_gain_hbm, ids_hbm, router_hbm, wg, wu, wd, out_ref,
-               x1_ref, mlp_gain, ids_ref, router_ref, gt_ref, ring, xall, xs, ybuf, pick, terms, part, dr, step1, step2, gtall,
-               ssem, wsem, a_send, a_recv, f_send, f_recv, d_send, d_recv, g_send, g_recv, p_send, p_recv, u_send, u_recv, w_send, w_recv):
+    )(pos, x, attn_gain, q_gain, k_gain, wq, wk, wv, wo, k_in, v_in, *prev, *ready)
+
+
+def moe_kernel(layer, follow, x1_hbm, mlp_gain_hbm, ids_hbm, router_hbm, wg, wu, wd, *rest):
+    if follow:
+        (pos_hbm, attn_gain_hbm, q_gain_hbm, k_gain_hbm, wq, wk, wv, out_ref, qkv_out,
+         pos_ref, attn_gain, q_gain, k_gain, angle, qsem, *rest) = rest
+    else:
+        out_ref, *rest = rest
+    (x1_ref, mlp_gain, ids_ref, router_ref, gt_ref, ring, xall, xs, ybuf, pick, terms, part, dr, step1, step2, gtall,
+               ssem, wsem, a_send, a_recv, f_send, f_recv, d_send, d_recv, g_send, g_recv, p_send, p_recv, u_send, u_recv, w_send, w_recv) = rest
     rows, dim = x1_ref.shape
     experts, _, ffn = wg.shape
     all_experts = router_ref.shape[0]
@@ -232,10 +262,23 @@
     def wait_weights(slot, part_of):
         pltpu.make_async_copy(wg.at[0], ring.at[slot, part_of], wsem.at[slot, part_of]).wait()
 
+    if follow:
+        late = [pltpu.make_async_copy(src, dst, qsem.at[n]) for n, (src, dst) in enumerate((
+            (pos_hbm, pos_ref), (attn_gain_hbm, attn_gain), (q_gain_hbm, q_gain), (k_gain_hbm, k_gain)))]
+        projections = (wq, wk, wv)
+
+    def start_projection(which, slot):
+        for j in range(2):
+            cols = pl.ds(j * ffn, ffn)
+            pltpu.make_async_copy(projections[which].at[layer + 1, :, cols], ring.at[slot, j], wsem.at[slot, j]).start(priority=1)
+
     small = [pltpu.make_async_copy(src, dst, ssem.at[n]) for n, (src, dst) in enumerate((
         (x1_hbm, x1_ref), (mlp_gain_hbm, mlp_gain), (ids_hbm, ids_ref), (router_hbm, router_ref)))]
     for copy in small:
         copy.start()
+    if follow:
+        for copy in late:
+            copy.start()
     for i in range(SLOTS):
         start_experts(i, i)
 
@@ -399,6 +442,12 @@
         @pl.when(jnp.logical_and(e + SLOTS >= experts, e + SLOTS < pairs))
         def _():
             start_down(e + SLOTS - experts, slot)
+
+        if follow:
+            for which in range(2):
+                @pl.when(e + SLOTS == pairs + which)
+                def _():
+                    start_projection(which, slot)
         return carry
 
     lax.fori_loop(0, experts, expert_step, 0)
@@ -457,6 +506,11 @@
                 for b in range(groups):
                     ybuf[b, e * CAP:(e + 1) * CAP, :] = rows_out[b * CAP:(b + 1) * CAP, :]
 
+        if follow:
+            @pl.when(c == per - 1)
+            def _():
+                start_projection(2, slot)
+
         @pl.when(jnp.logical_and(c >= 1, c <= blocks))
         def _():
             relay_pair(c - 1)
@@ -491,9 +545,46 @@
             for k in range(2):
                 first_copy(c, s, k).wait_send()
             second_copy(c, s).wait_send()
-
-
-def moe(layer, x1, mlp_gain, ids, router_t, wg, wu, wd, groups, out_type):
+    if follow:
+        for copy in late:
+            copy.wait()
+        heads = dim // 128
+        at_rows = pl.ds(0, rows)
+        xall[at_rows, :] = rms_rows(out_ref[...].astype(F32), attn_gain[layer + 1:layer + 2, :]).astype(BF16)
+        cos, sin = rotary(angle, pos_ref, rows, 128)
+        leaving = []
+        for which in range(3):
+            slot = (pairs + which) % SLOTS
+            for j in range(2):
+                wait_weights(slot, j)
+                for n in range(0, ffn, ACOLS):
+                    values = jnp.dot(xall[at_rows, :], ring[slot, j, :, n:n + ACOLS], preferred_element_type=F32)
+                    if which == 2:
+                        xs[which, at_rows, j * ffn + n:j * ffn + n + ACOLS] = values.astype(BF16)
+                        continue
+                    for i in range(ACOLS // 128):
+                        h = (j * ffn + n) // 128 + i
+                        step1[h // 4, h // 2 % 2, h % 2] = values[:, i * 128:(i + 1) * 128]
+            if which < 2:
+                gain_ref = (q_gain, k_gain)[which]
+                square = sum(step1[h // 4, h // 2 % 2, h % 2] ** 2 for h in range(heads))
+                inv_rms = lax.rsqrt(jnp.sum(square, axis=-1, keepdims=True) / dim + RMS_EPS)
+                for h in range(heads):
+                    cols = slice(h * 128, (h + 1) * 128)
+                    turned = step1[h // 4, h // 2 % 2, h % 2] * inv_rms * gain_ref[layer + 1:layer + 2, cols]
+                    turned = turned * cos + pltpu.roll(turned, 64, 1) * sin
+                    xs[which, at_rows, cols] = turned.astype(BF16)
+            leaving.append(pltpu.make_async_copy(xs.at[which, at_rows], qkv_out.at[which], qsem.at[4 + which]))
+            if which:
+                leaving[which - 1].start()
+    if follow:
+        leaving[2].start()
+    if follow:
+        for copy in leaving:
+            copy.wait()
+
+
+def moe(layer, x1, mlp_gain, ids, router_t, wg, wu, wd, groups, follow):
     rows, dim = x1.shape
     experts, _, ffn = wg.shape
     slots = CAP * groups
@@ -502,12 +593,14 @@
     chips = groups // 2
     dma = pltpu.SemaphoreType.DMA
     return pl.pallas_call(
-        functools.partial(moe_kernel, layer),
+        functools.partial(moe_kernel, layer, bool(follow)),
         name="moe",
-        out_shape=jax.ShapeDtypeStruct((rows, dim), out_type),
-        in_specs=[ANY] * 7,
-        out_specs=VMEM,
+        out_shape=(jax.ShapeDtypeStruct((rows, dim), BF16),) + ((jax.ShapeDtypeStruct((3, rows, dim), BF16),) if follow else ()),
+        in_specs=[ANY] * (7 + len(follow)),
+        out_specs=(VMEM, ANY) if follow else (VMEM,),
         scratch_shapes=[
+            *([pltpu.SMEM(follow[0].shape, follow[0].dtype), *[pltpu.VMEM(a.shape, a.dtype) for a in follow[1:4]],
+               pltpu.VMEM((rows, 128), F32), dma((7,))] if follow else []),
             *[pltpu.VMEM(a.shape, a.dtype) for a in (x1, mlp_gain, ids, router_t)],
             pltpu.VMEM((router_t.shape[0], 128), F32),
             pltpu.VMEM((SLOTS, 2, dim, ffn), BF16),
@@ -526,7 +619,7 @@
             dma((blocks,)), dma((blocks,)), dma((blocks, 2, 2)), dma((blocks, 2, 2)), dma((blocks, 2)), dma((blocks, 2)),
         ],
         compiler_params=pltpu.CompilerParams(collective_id=layer, has_side_effects=True, vmem_limit_bytes=67043328),
-    )(x1, mlp_gain, ids, router_t, wg, wu, wd)
+    )(x1, mlp_gain, ids, router_t, wg, wu, wd, *follow)
 
 
 def solution(mesh):
@@ -537,13 +630,14 @@
         ids = jnp.transpose(expert_ids, (0, 2, 1))
         router_t = w_router.T
         caches = None
+        ready = ()
         for layer in range(expert_ids.shape[0]):
             x1, k_new, v_new = attention(layer, positions, hidden, attn_gain, q_gain, k_gain,
-                                         w_query, w_key, w_value, w_out, k_cache, v_cache, caches)
+                                         w_query, w_key, w_value, w_out, k_cache, v_cache, caches, ready)
             caches = (k_new, v_new)
-            out_type = BF16
-            hidden = moe(layer, x1, mlp_gain, ids, router_t, w_gate, w_up, w_down, groups, out_type)
-        return hidden.astype(BF16), caches[0], caches[1]
+            follow = () if layer + 1 == expert_ids.shape[0] else (positions, attn_gain, q_gain, k_gain, w_query, w_key, w_value)
+            hidden, *ready = moe(layer, x1, mlp_gain, ids, router_t, w_gate, w_up, w_down, groups, follow)
+        return hidden, caches[0], caches[1]
 
     row_spec = P(batch_axes, None)
     cache_spec = P(None, batch_axes, None, None, None)

time: 140 us -> 140 us (level)
  no operation moved by 1% of the time
where the time goes in v4:
time: 140 us
  Pallas kernels  138 us (99%)
  local copies, waits for them, and re-layouts  1.67 us (1%)
    pallas_call x2, Pallas kernels, moe(): pl.pallas_call(functools.partial(moe_kernel, layer, bool(follow)), name='...  108 us
    pallas_call x2, Pallas kernels, attention(): pl.pallas_call(functools.partial(attn_kernel, layer, bool(ready)), name='...  29.6 us

profile of v4, /device:TPU:0, one launch (start us, length us, event | category | flops | bytes accessed | tf_op | source)
XLA Modules:
  0.0 140.0 jit_solution(17722237058036639505)
XLA Ops:
  0.6 18.2 %attn.2 = (bf16[64,2048]{1,0:T(8,128)(2,1)}, bf16[2,64,16,16,128]{4,3,2,1,0:T(8,128)(2,1)}, bf16[2,64,16,16,128]{4,3,2,1,0:T(8,128)(2,1)}) custom-call(s32[64]{0:T(128)} %pos_hbm.3, bf16[64,2048]{1,0:T(8,128)(2,1)} %x_hbm.1, f32[2,2048]{1,0:T(2,128)} %attn_gain_hbm.3, f32[2,2048]{1,0:T(2,128)} %q_gain_hbm.3, f32[2,2048]{1,0:T(2,128)} %k_gain_hbm.3, ...), custom_call_target="tpu_custom_call" | custom-call | tf_op jit(solution)/shard_map/attn/pallas_call | solution.py:193
  18.8 58.8 %moe.2 = (bf16[64,2048]{1,0:T(8,128)(2,1)}, bf16[3,64,2048]{2,1,0:T(8,128)(2,1)}) custom-call(bf16[64,2048]{1,0:T(8,128)(2,1)} %get-tuple-element.11.x1_hbm, f32[2,2048]{1,0:T(2,128)} %mlp_gain_hbm.3, s32[2,8,64]{2,1,0:T(8,128)} %bitcast.4, bf16[64,2048]{1,0:T(8,128)(2,1)} %bitcast.2, bf16[8,2048,1024]{2,1,0:T(8,128)(2,1)} %wg.3, bf16[8,2048,1024]{2,1,0:T(8,128)(2,1)} %wu.3, ...), custom_call_target="tpu_custom_call" | custom-call | tf_op jit(solution)/shard_map/moe/pallas_call | solution.py:595
  77.6 11.4 %attn.3 = (bf16[64,2048]{1,0:T(8,128)(2,1)}, bf16[2,64,16,16,128]{4,3,2,1,0:T(8,128)(2,1)}, bf16[2,64,16,16,128]{4,3,2,1,0:T(8,128)(2,1)}) custom-call(s32[64]{0:T(128)} %pos_hbm.3, bf16[64,2048]{1,0:T(8,128)(2,1)} %get-tuple-element.12.x_hbm, f32[2,2048]{1,0:T(2,128)} %attn_gain_hbm.3, ...), custom_call_target="tpu_custom_call", output_to_operand_aliasing={{1}: (11, {}), {2}: (12, {})} | custom-call | tf_op jit(solution)/shard_map/attn/pallas_call | solution.py:193
  89.0 49.3 %moe.3 = bf16[64,2048]{1,0:T(8,128)(2,1)} custom-call(bf16[64,2048]{1,0:T(8,128)(2,1)} %get-tuple-element.16.x1_hbm, f32[2,2048]{1,0:T(2,128)} %mlp_gain_hbm.3, s32[2,8,64]{2,1,0:T(8,128)} %bitcast.5, bf16[64,2048]{1,0:T(8,128)(2,1)} %bitcast.3, bf16[8,2048,1024]{2,1,0:T(8,128)(2,1)} %wg.3, bf16[8,2048,1024]{2,1,0:T(8,128)(2,1)} %wu.3, bf16[8,1024,2048]{2,1,0:T(8,128)(2,1)} %wd.3), custom_call_target="tpu_custom_call" | custom-call | tf_op jit(solution)/shard_map/moe/pallas_call | solution.py:595
  138.3 1.7 %copy.25 = bf16[64,2048]{1,0:T(8,128)(2,1)} copy(bf16[64,2048]{1,0:T(8,128)(2,1)} %moe.3) | data formatting | bytes 524288
